TPU v7x, 8 devices: a whole 2x2x1 slice. The times are simulated.
8 devices in a mesh: data: 8 (over z, y, x, core).
Axes of the slice: x: 2, y: 2, z: 1, core: 2. Of those that a mesh axis runs over, the one named last changes fastest.
Arguments:
- grad_attn: bfloat16 [8, 12, 1048576], P('data')
- grad_mlp: bfloat16 [8, 6, 4194304], P('data')
- grad_wide: bfloat16 [8, 3, 4096], P('data')
- grad_vec: bfloat16 [8, 29, 1024], P('data')
- weight_attn: float32 [12, 1048576], P(None, 'data')
- weight_mlp: float32 [6, 4194304], P(None, 'data')
- weight_wide: float32 [3, 4096], P(None, 'data')
- weight_vec: float32 [29, 1024], P(None, 'data')
- mom1_attn: float32 [12, 1048576], P(None, 'data')
- mom1_mlp: float32 [6, 4194304], P(None, 'data')
- mom1_wide: float32 [3, 4096], P(None, 'data')
- mom1_vec: float32 [29, 1024], P(None, 'data')
- mom2_attn: float32 [12, 1048576], P(None, 'data')
- mom2_mlp: float32 [6, 4194304], P(None, 'data')
- mom2_wide: float32 [3, 4096], P(None, 'data')
- mom2_vec: float32 [29, 1024], P(None, 'data')
Outputs:
- output 1: bfloat16 [12, 1048576], replicated
- output 2: bfloat16 [6, 4194304], replicated
- output 3: bfloat16 [3, 4096], replicated
- output 4: bfloat16 [29, 1024], replicated
- output 5: float32 [12, 1048576], P(None, 'data')
- output 6: float32 [6, 4194304], P(None, 'data')
- output 7: float32 [3, 4096], P(None, 'data')
- output 8: float32 [29, 1024], P(None, 'data')
- output 9: float32 [12, 1048576], P(None, 'data')
- output 10: float32 [6, 4194304], P(None, 'data')
- output 11: float32 [3, 4096], P(None, 'data')
- output 12: float32 [29, 1024], P(None, 'data')
- output 13: float32 [12, 1048576], P(None, 'data')
- output 14: float32 [6, 4194304], P(None, 'data')
- output 15: float32 [3, 4096], P(None, 'data')
- output 16: float32 [29, 1024], P(None, 'data')
All inputs are finite; a program needn't handle non-finite values.
Results may differ from a plain program's by a relative error of at most 0.001.
Values are sent between devices in bfloat16 or wider.
A program may use at most 1 GiB of HBM per device.

v0:
```python
import jax
import jax.numpy as jnp
from jax import lax
from jax.sharding import PartitionSpec as P

STEP_NUMBER = 10
LEARN_RATE = 0.04
BETA_FIRST = 0.9
BETA_SECOND = 0.999
EPSILON = 1e-6
WEIGHT_DECAY = 0.01
MAX_NORM = 1.0


def adam_direction(mean_grad, weight, first_moment, second_moment, clip_coef):
    clipped = clip_coef * mean_grad
    new_first = BETA_FIRST * first_moment + (1.0 - BETA_FIRST) * clipped
    new_second = BETA_SECOND * second_moment + (1.0 - BETA_SECOND) * (clipped * clipped)
    update = (new_first / (1.0 - BETA_FIRST ** STEP_NUMBER)) / (jnp.sqrt(new_second / (1.0 - BETA_SECOND ** STEP_NUMBER)) + EPSILON) + WEIGHT_DECAY * weight
    return update, new_first, new_second


def solution(mesh):
    group_size = mesh.shape["data"]
    grad_spec = P("data", None, None)
    shard_spec = P(None, "data")
    full_spec = P(None, None)

    def local_step(*all_banks):
        grad_banks = all_banks[0:4]
        weights = all_banks[4:8]
        firsts = all_banks[8:12]
        seconds = all_banks[12:16]
        mean_grads = []
        for grad_bank in grad_banks:
            row_count = grad_bank.shape[1]
            shard_width = grad_bank.shape[2] // group_size
            by_owner = grad_bank.reshape(row_count, group_size, shard_width)
            received = lax.all_to_all(by_owner, "data", 1, 1, tiled=True)
            mean_grads.append(jnp.sum(received, axis=1, dtype=jnp.float32) / group_size)
        local_square = sum(jnp.sum(mean_grad * mean_grad) for mean_grad in mean_grads)
        clip_coef = jnp.minimum(1.0, MAX_NORM / jnp.sqrt(lax.psum(local_square, "data")))
        results = [adam_direction(mean_grads[bank_index], weights[bank_index], firsts[bank_index], seconds[bank_index], clip_coef) for bank_index in range(4)]
        part_sums = jnp.concatenate([jnp.sum(weight * weight, axis=1) for weight in weights] + [jnp.sum(result[0] * result[0], axis=1) for result in results])
        norm_sums = lax.psum(part_sums, "data")
        tensor_count = norm_sums.shape[0] // 2
        trust_ratios = jnp.sqrt(norm_sums[:tensor_count]) / jnp.sqrt(norm_sums[tensor_count:])
        replicas, new_weights = [], []
        first_row = 0
        for bank_index in range(4):
            row_count = weights[bank_index].shape[0]
            trust_ratio = trust_ratios[first_row:first_row + row_count]
            first_row = first_row + row_count
            new_weight = weights[bank_index] - LEARN_RATE * trust_ratio[:, None] * results[bank_index][0]
            new_weights.append(new_weight)
            replicas.append(lax.all_gather(new_weight.astype(jnp.bfloat16), "data", axis=1, tiled=True))
        return tuple(replicas + new_weights + [result[1] for result in results] + [result[2] for result in results])

    return jax.shard_map(local_step, mesh=mesh, in_specs=(grad_spec,) * 4 + (shard_spec,) * 12, out_specs=(full_spec,) * 4 + (shard_spec,) * 12, check_vma=False)
```

profile of v0, /device:TPU:0, one launch (start us, length us, event | category | flops | bytes accessed | tf_op | source)
XLA Modules:
  0.0 1897.1 jit_solution(15581255777378901235)
XLA Ops:
  7.2 4.3 all-to-all-start.2
  11.5 0.8 copy.35
  12.4 0.6 copy.33
  13.0 3.1 all-to-all-done.2
  16.1 2.1 all-to-all-start.3
  18.2 29.3 %copy.34 = bf16[2,8,8,131072]{3,2,1,0:T(8,128)(2,1)} copy(bf16[2,8,8,131072]{3,1,2,0:T(8,128)(2,1)} %bitcast.11) | data formatting | bytes 67108864
  47.5 20.5 %slice.24 = bf16[12,8,131072]{2,1,0:T(8,128)(2,1)} slice(bf16[16,8,131072]{2,1,0:T(8,128)(2,1)} %bitcast.10), slice={[0:12], [0:8], [0:131072]} | slice | bytes 50331648 | tf_op jit(solution)/shard_map/reshape | solution.py:38
  68.0 24.7 %copy.32 = bf16[12,8,131072]{2,0,1:T(8,128)(2,1)} copy(bf16[12,8,131072]{2,1,0:T(8,128)(2,1)} %slice.24) | data formatting | bytes 50331648 | tf_op jit(solution)/shard_map/reshape | solution.py:38
  92.7 373.3 %all_to_all.20 = bf16[12,8,131072]{2,0,1:T(8,128)(2,1)} all-to-all(bf16[12,8,131072]{2,0,1:T(8,128)(2,1)} %copy.32), channel_id=1, replica_groups=mesh['data'=8] {'data'}, dimensions={1} | all-to-all | bytes 50331648 | tf_op jit(solution)/shard_map/all_to_all | solution.py:39
  466.0 8.6 all-to-all-start.1
  474.5 0.0 all-gather.3.cloned.1.call-start
  474.6 0.6 multiply_reduce_fusion.10
  475.2 0.6 multiply_reduce_fusion.7
  475.9 15.2 convert_reduce_fusion.1
  491.1 6.1 multiply_reduce_fusion.4
  497.2 701.1 %all-to-all-done.1 = bf16[6,8,524288]{2,0,1:T(8,128)(2,1)} async-done(((bf16[6,8,524288]{2,0,1:T(8,128)(2,1)}), bf16[6,8,524288]{2,0,1:T(8,128)(2,1)}, u32[]{:S(2)}, u32[]{:S(2)}) %all-to-all-start.1) | async-done | bytes 50331680 | tf_op jit(solution)/shard_map/all_to_all | solution.py:39
  1198.3 36.5 %convert_reduce_fusion = f32[6,524288]{1,0:T(8,128)S(1)} fusion(bf16[6,8,524288]{2,0,1:T(8,128)(2,1)} %all-to-all-done.1), kind=kLoop, calls=%fused_computation | loop fusion | flops 47185920 | bytes 62914560 | tf_op jit(solution)/shard_map/reduce_sum | solution.py:40
  1234.8 0.0 copy-start
  1234.8 6.2 copy-done
  1241.0 4.9 multiply_reduce_fusion.1
  1248.5 22.4 %psum.14 = f32[]{:T(128)} all-reduce(f32[]{:T(128)S(6)} %add.75), channel_id=1, replica_groups=mesh['data'=8] {'data'}, use_global_device_ids=true, to_apply=%region_12.0 | all-reduce | flops 1 | bytes 8 | tf_op jit(solution)/shard_map/psum | solution.py:42
  1271.7 0.8 multiply_reduce_fusion.9
  1272.4 33.7 %multiply_reduce_fusion = (f32[6]{0:T(128)S(1)}, f32[6]{0:T(128)S(1)}, f32[6,524288]{1,0:T(8,128)}, f32[6,524288]{1,0:T(8,128)}) fusion(f32[6,524288]{1,0:T(8,128)} %param.21, f32[6,524288]{1,0:T(8,128)} %copy-done, f32[]{:T(128)S(6)} %mul.252, f32[6,524288]{1,0:T(8,128)} %param.25, f32[6,524288]{1,0:T(8,128)} %param.29), kind=kLoop, calls=%fused_computation.3 | loop fusion | flops 56623088 | bytes 75497520 | tf_op jit(solution)/shard_map/reduce_sum | solution.py:44
  1306.1 0.0 copy-start.5
  1306.2 20.2 %multiply_reduce_fusion.3 = (f32[12]{0:T(128)S(1)}, f32[12]{0:T(128)S(1)}, f32[12,131072]{1,0:T(8,128)}, f32[12,131072]{1,0:T(8,128)}) fusion(f32[12,131072]{1,0:T(8,128)} %param.20, f32[12,131072]{1,0:T(8,128)} %convert_reduce_fusion.1, f32[]{:T(128)S(6)} %mul.252, f32[12,131072]{1,0:T(8,128)} %param.24, f32[12,131072]{1,0:T(8,128)} %param.28), kind=kLoop, calls=%fused_computation.10 | loop fusion | flops 28311528 | bytes 37748836 | tf_op jit(solution)/shard_map/reduce_sum | solution.py:44
  1326.4 0.1 multiply_reduce_fusion.6
  1326.5 0.0 copy-start.3
  1326.5 0.1 concatenate.3
  1326.6 23.2 %psum.15 = f32[100]{0:T(128)S(1)} all-reduce(f32[100]{0:T(128)S(1)} %concatenate.3), channel_id=1, replica_groups=mesh['data'=8] {'data'}, use_global_device_ids=true, to_apply=%region_17.0 | all-reduce | flops 100 | bytes 800 | tf_op jit(solution)/shard_map/psum | solution.py:45
  1349.8 0.1 rsqrt_multiply_fusion
  1349.9 0.1 slice_multiply_fusion.2
  1350.0 14.0 fusion.3
  1363.9 0.0 all-gather.3.cloned.1.call-update
  1363.9 0.3 all-gather.5.cloned.1.call-start
  1364.2 25.5 %fusion.2 = (bf16[6,524288]{1,0:T(8,128)(2,1)}, f32[6,524288]{1,0:T(8,128)}) fusion(f32[6,524288]{1,0:T(8,128)} %param.21, f32[6,524288]{1,0:T(8,128)} %get-tuple-element.70, f32[6,524288]{1,0:T(8,128)} %get-tuple-element.66, f32[6]{0:T(128)S(1)} %slice_multiply_fusion.2), kind=kLoop, calls=%fused_computation.39 | loop fusion | flops 28311552 | bytes 56623128 | tf_op jit(solution)/shard_map/convert_element_type | solution.py:56
  1389.8 0.0 all-gather.5.cloned.1.call-update
  1389.8 0.1 slice_multiply_fusion
  1389.9 0.7 fusion
  1390.5 13.3 all_gather.15
  1403.8 0.1 slice_multiply_fusion.1
  1403.9 0.7 fusion.1
  1404.6 11.6 all_gather.14
  1416.2 106.0 %all-gather.3.cloned.1.call-done = bf16[12,1048576]{1,0:T(8,128)(2,1)} async-done(((bf16[12,131072]{1,0:T(8,128)(2,1)}), bf16[12,1048576]{1,0:T(8,128)(2,1)}) %all-gather.3.cloned.1.call-update) | async-done | bytes 25165840 | tf_op jit(solution)/shard_map/all_gather | solution.py:56
  1522.2 299.6 %all-gather.5.cloned.1.call-done = bf16[6,4194304]{1,0:T(8,128)(2,1)} async-done(((bf16[6,524288]{1,0:T(8,128)(2,1)}), bf16[6,4194304]{1,0:T(8,128)(2,1)}) %all-gather.5.cloned.1.call-update) | async-done | bytes 50331664 | tf_op jit(solution)/shard_map/all_gather | solution.py:56
  1821.9 22.9 %copy.40 = bf16[12,1048576]{1,0:T(8,128)(2,1)} copy(bf16[12,1048576]{1,0:T(8,128)(2,1)} %all-gather.3.cloned.1.call-done) | data formatting | bytes 50331648
  1844.7 44.3 %copy.41 = bf16[6,4194304]{1,0:T(8,128)(2,1)} copy(bf16[6,4194304]{1,0:T(8,128)(2,1)} %all-gather.5.cloned.1.call-done) | data formatting | bytes 100663296
  1889.0 0.6 copy.42
  1889.6 0.6 copy.43
  (19 shorter events, 0.1 us)
Async XLA Ops:
  7.2 8.9 all-to-all-start.2
  16.1 76.6 %all-to-all-start.3 = ((bf16[29,8,128]{2,0,1:T(8,128)(2,1)}), bf16[29,8,128]{2,0,1:T(8,128)(2,1)S(1)}, u32[]{:S(2)}, u32[]{:S(2)}) async-start(bf16[29,8,128]{2,0,1:T(8,128)(2,1)} %copy.33), calls=%async_computation.3 | async-start | bytes 131072 | tf_op jit(solution)/shard_map/all_to_all | solution.py:39
  466.0 732.3 %all-to-all-start.1 = ((bf16[6,8,524288]{2,0,1:T(8,128)(2,1)}), bf16[6,8,524288]{2,0,1:T(8,128)(2,1)}, u32[]{:S(2)}, u32[]{:S(2)}) async-start(bf16[6,8,524288]{2,0,1:T(8,128)(2,1)} %bitcast), calls=%async_computation.1 | async-start | bytes 134217728 | tf_op jit(solution)/shard_map/all_to_all | solution.py:39
  474.5 1047.7 %all-gather.3.cloned.1.call-start = ((), (), s32[]{:S(2)}) async-start(), calls=%async_computation.4 | async-start | bytes 37748736 | tf_op jit(solution)/shard_map/all_gather | solution.py:56
  1234.8 6.2 copy-start
  1241.0 30.7 %copy-start.4 = (f32[3,512]{1,0:T(4,128)S(1)}, f32[3,512]{1,0:T(4,128)}, u32[]{:S(2)}) copy-start(f32[3,512]{1,0:T(4,128)} %param.22) | copy-start | bytes 18436
  1241.0 30.7 %copy-start.7 = (f32[3,512]{1,0:T(4,128)S(1)}, f32[3,512]{1,0:T(4,128)}, u32[]{:S(2)}) copy-start(f32[3,512]{1,0:T(4,128)} %param.26) | copy-start | bytes 18436
  1241.0 30.7 %copy-start.8 = (f32[3,512]{1,0:T(4,128)S(1)}, f32[3,512]{1,0:T(4,128)}, u32[]{:S(2)}) copy-start(f32[3,512]{1,0:T(4,128)} %param.30) | copy-start | bytes 18436
  1306.1 20.2 %copy-start.1 = (f32[29,128]{1,0:T(8,128)S(1)}, f32[29,128]{1,0:T(8,128)}, u32[]{:S(2)}) copy-start(f32[29,128]{1,0:T(8,128)} %param.23) | copy-start | bytes 44548
  1306.1 20.2 %copy-start.5 = (f32[29,128]{1,0:T(8,128)S(1)}, f32[29,128]{1,0:T(8,128)}, u32[]{:S(2)}) copy-start(f32[29,128]{1,0:T(8,128)} %param.27) | copy-start | bytes 44548
  1306.2 20.2 %copy-start.6 = (f32[29,128]{1,0:T(8,128)S(1)}, f32[29,128]{1,0:T(8,128)}, u32[]{:S(2)}) copy-start(f32[29,128]{1,0:T(8,128)} %param.31) | copy-start | bytes 44548
  1326.5 63.3 %copy-start.2 = (f32[29,128]{1,0:T(8,128)}, f32[29,128]{1,0:T(8,128)S(1)}, u32[]{:S(2)}) copy-start(f32[29,128]{1,0:T(8,128)S(1)} %get-tuple-element.68) | copy-start | bytes 44548
  1326.5 63.3 %copy-start.3 = (f32[29,128]{1,0:T(8,128)}, f32[29,128]{1,0:T(8,128)S(1)}, u32[]{:S(2)}) copy-start(f32[29,128]{1,0:T(8,128)S(1)} %get-tuple-element.72) | copy-start | bytes 44548
  1363.9 457.9 %all-gather.5.cloned.1.call-start = ((), (), s32[]{:S(2)}) async-start(), calls=%async_computation.5 | async-start | bytes 75497472 | tf_op jit(solution)/shard_map/all_gather | solution.py:56
Sparse Core Ops, SparseCore 0:
  1364.1 158.1 all-gather.2
  1524.6 297.1 all-gather.4
where the time goes:
time: 1900 us
  waiting for transfers between devices  1110 us (58%)
  blocking collectives  444 us (23%)
  other arithmetic  160 us (8%)
  local copies, waits for them, and re-layouts  151 us (8%)
    all_to_all x3, waiting for transfers between devices, local_step(): received = lax.all_to_all(by_owner, 'data', 1, 1, tiled=True)  704 us
    all_gather x2, waiting for transfers between devices, local_step(): lax.all_gather(new_weight.astype(jnp.bfloat16), 'data', axis=1, tiled=True)  406 us
    all_to_all x1, blocking collectives, local_step(): received = lax.all_to_all(by_owner, 'data', 1, 1, tiled=True)  373 us
    unnamed x24, local copies, waits for them, and re-layouts  105 us
    reduce_sum x4, other arithmetic, local_step(): jnp.sum(result[0] * result[0], axis=1)  54.8 us
    reduce_sum x4, other arithmetic, local_step(): mean_grads.append(jnp.sum(received, axis=1, dtype=jnp.float32) / group_size)  51.8 us
    reshape x4, local copies, waits for them, and re-layouts, local_step(): by_owner = grad_bank.reshape(row_count, group_size, shard_width)  45.9 us
    convert_element_type x4, other arithmetic, local_step(): new_weight.astype(jnp.bfloat16)  40.8 us
  transfers between devices with their start and end apart: 5, of which 4 were waited for; matrix products, arithmetic and copies ran while one was open for 7% of the time, Pallas kernels for 0%

commit v1 on v0

--- a/solution.py
+++ b/solution.py
@@ -1,6 +1,10 @@
+import functools
+
 import jax
 import jax.numpy as jnp
 from jax import lax
+from jax.experimental import pallas as pl
+from jax.experimental.pallas import tpu as pltpu
 from jax.sharding import PartitionSpec as P
 
 STEP_NUMBER = 10
@@ -11,6 +15,281 @@
 WEIGHT_DECAY = 0.01
 MAX_NORM = 1.0
 
+MESH = pl.DeviceIdType.MESH
+SLOTS = 8
+AHEAD = 2
+LAG_ONE = 4
+LAG_TWO = 8
+ATTN_WIDTH = 1024
+
+
+def signal_all_and_wait(me, devices):
+    barrier = pltpu.get_barrier_semaphore()
+    for step in range(1, devices):
+        pl.semaphore_signal(barrier, inc=1, device_id=(lax.rem(me + step, devices),), device_id_type=MESH)
+    pl.semaphore_wait(barrier, devices - 1)
+
+
+def share_tile(me, devices, tiles, send_sem, recv_sem):
+    copies = []
+    for step in range(1, devices):
+        other = lax.rem(me + step, devices)
+        copy = pltpu.make_async_remote_copy(
+            src_ref=tiles.at[me], dst_ref=tiles.at[me], send_sem=send_sem.at[step], recv_sem=recv_sem.at[step],
+            device_id=(other,), device_id_type=MESH)
+        copy.start()
+        copies.append(copy)
+    for copy in copies:
+        copy.wait()
+
+
+def scatter_kernel(devices, widths, chunks, ga, gm, gw, gv, oa, om, ow, ov, total,
+                   la, lm, pa, pm, s1a, s1m, r1a, r1m, s2a, s2m, r2a, r2m, ba, bm, rw, rv, sqa, sqm, tiles,
+                   load_sem, psend_sem, precv_sem, send1_sem, recv1_sem, send2_sem, recv2_sem, out_sem,
+                   wsend_sem, wrecv_sem, vsend_sem, vrecv_sem, tsend_sem, trecv_sem, pcredit, credit1, credit2):
+    me = lax.axis_index("data")
+    core = lax.rem(me, 2)
+    x = lax.rem(me // 2, 2)
+    y = me // 4
+    partner = me + 1 - 2 * core
+    xn = y * 4 + (1 - x) * 2 + core
+    yn = (1 - y) * 4 + x * 2 + core
+    banks = ((ga, oa, la, pa, s1a, r1a, s2a, r2a, ba, sqa, widths[0]), (gm, om, lm, pm, s1m, r1m, s2m, r2m, bm, sqm, widths[1]))
+
+    signal_all_and_wait(me, devices)
+
+    small = []
+    for step in range(1, devices):
+        other = lax.rem(me + step, devices)
+        for src, dst, ssem, rsem in ((gw, rw, wsend_sem, wrecv_sem), (gv, rv, vsend_sem, vrecv_sem)):
+            width = dst.shape[2]
+            copy = pltpu.make_async_remote_copy(
+                src_ref=src.at[0, :, pl.ds(pl.multiple_of(other * width, width), width)], dst_ref=dst.at[step],
+                send_sem=ssem.at[step], recv_sem=rsem.at[step], device_id=(other,), device_id_type=MESH)
+            copy.start()
+            small.append(copy)
+
+    sqa[...] = jnp.zeros_like(sqa)
+    sqm[...] = jnp.zeros_like(sqm)
+
+    def column(kind, chip_x, chip_y, owner_core, bank_length, width, chunk):
+        owner = chip_y * 4 + chip_x * 2 + owner_core
+        return pl.multiple_of(owner * bank_length + chunk * width, width)
+
+    def chips(kind):
+        fx, fy = x + kind * (1 - 2 * x), y + (1 - kind) * (1 - 2 * y)
+        nx, ny = x + (1 - kind) * (1 - 2 * x), y + kind * (1 - 2 * y)
+        return ((x, y), (fx, fy), (nx, ny), (1 - x, 1 - y))
+
+    def first_peer(kind):
+        return xn + kind * (yn - xn)
+
+    def second_peer(kind):
+        return yn + kind * (xn - yn)
+
+    def send_one(slot, kind, bank):
+        s1, r1 = banks[bank][4], banks[bank][5]
+        return pltpu.make_async_remote_copy(
+            src_ref=s1.at[slot], dst_ref=r1.at[slot], send_sem=send1_sem.at[bank, slot], recv_sem=recv1_sem.at[bank, slot],
+            device_id=(first_peer(kind),), device_id_type=MESH)
+
+    def send_two(slot, kind, bank):
+        s2, r2 = banks[bank][6], banks[bank][7]
+        return pltpu.make_async_remote_copy(
+            src_ref=s2.at[slot], dst_ref=r2.at[slot], send_sem=send2_sem.at[bank, slot], recv_sem=recv2_sem.at[bank, slot],
+            device_id=(second_peer(kind),), device_id_type=MESH)
+
+    def out_copy(chunk, slot, bank):
+        out, staged, width = banks[bank][1], banks[bank][8], banks[bank][10]
+        return pltpu.make_async_copy(staged.at[slot], out.at[:, pl.ds(pl.multiple_of(chunk * width, width), width)], out_sem.at[bank, slot])
+
+    def body(i, carry):
+        d = i - AHEAD - LAG_TWO
+
+        @pl.when(d >= 0)
+        def _():
+            slot = lax.rem(d, SLOTS)
+            kind = lax.rem(d, 2)
+            for bank in range(2):
+                r2, staged, sq, width = banks[bank][7], banks[bank][8], banks[bank][9], banks[bank][10]
+                one, two = send_one(slot, kind, bank), send_two(slot, kind, bank)
+                two.wait_recv()
+                one.wait_send()
+                two.wait_send()
+                square = sq[...]
+                for at in range(0, width, 128):
+                    mean = (staged[slot, :, at:at + 128] + r2[slot, :, at:at + 128]) * (1.0 / devices)
+                    staged[slot, :, at:at + 128] = mean
+                    square = square + mean * mean
+                sq[...] = square
+                out_copy(d, slot, bank).start()
+
+            @pl.when(d + SLOTS < chunks)
+            def _():
+                pl.semaphore_signal(credit2.at[kind], inc=1, device_id=(second_peer(kind),), device_id_type=MESH)
+
+        c = i - AHEAD - LAG_ONE
+
+        @pl.when(jnp.logical_and(c >= 0, c < chunks))
+        def _():
+            slot = lax.rem(c, SLOTS)
+            kind = lax.rem(c, 2)
+
+            @pl.when(c >= SLOTS)
+            def _():
+                pl.semaphore_wait(credit2.at[kind], 1)
+
+            for bank in range(2):
+                l, p, r1, s2, staged = banks[bank][2], banks[bank][3], banks[bank][5], banks[bank][6], banks[bank][8]
+                send_one(slot, kind, bank).wait_recv()
+                pltpu.make_async_copy(p.at[slot], p.at[slot], psend_sem.at[bank, slot]).wait()
+
+                @pl.when(c >= SLOTS)
+                def _():
+                    out_copy(c - SLOTS, slot, bank).wait()
+
+                s2[slot] = r1[slot, 1] + (l[slot, 1].astype(jnp.float32) + p[slot, 1].astype(jnp.float32))
+                send_two(slot, kind, bank).start()
+                staged[slot] = r1[slot, 0] + (l[slot, 0].astype(jnp.float32) + p[slot, 0].astype(jnp.float32))
+
+            @pl.when(c + SLOTS < chunks)
+            def _():
+                pl.semaphore_signal(pcredit, inc=1, device_id=(partner,), device_id_type=MESH)
+                pl.semaphore_signal(credit1.at[kind], inc=1, device_id=(first_peer(kind),), device_id_type=MESH)
+
+        b = i - AHEAD
+
+        @pl.when(jnp.logical_and(b >= 0, b < chunks))
+        def _():
+            slot = lax.rem(b, SLOTS)
+            kind = lax.rem(b, 2)
+
+            @pl.when(b >= SLOTS)
+            def _():
+                pl.semaphore_wait(credit1.at[kind], 1)
+
+            for bank in range(2):
+                l, p, s1 = banks[bank][2], banks[bank][3], banks[bank][4]
+                pltpu.make_async_copy(l.at[slot], l.at[slot], load_sem.at[bank, slot]).wait()
+                pltpu.make_async_copy(p.at[slot], p.at[slot], precv_sem.at[bank, slot]).wait()
+                for block in range(2):
+                    s1[slot, block] = l[slot, 2 + block].astype(jnp.float32) + p[slot, 2 + block].astype(jnp.float32)
+                send_one(slot, kind, bank).start()
+
+        @pl.when(i < chunks)
+        def _():
+            slot = lax.rem(i, SLOTS)
+            kind = lax.rem(i, 2)
+
+            @pl.when(i >= SLOTS)
+            def _():
+                pl.semaphore_wait(pcredit, 1)
+
+            for bank in range(2):
+                g, l, p, width = banks[bank][0], banks[bank][2], banks[bank][3], banks[bank][10]
+                length = g.shape[2] // devices
+                for block, (bx, by) in enumerate(chips(kind)):
+                    theirs = column(kind, bx, by, 1 - core, length, width, i)
+                    pltpu.make_async_remote_copy(
+                        src_ref=g.at[0, :, pl.ds(theirs, width)], dst_ref=p.at[slot, block],
+                        send_sem=psend_sem.at[bank, slot], recv_sem=precv_sem.at[bank, slot],
+                        device_id=(partner,), device_id_type=MESH).start()
+                    mine = column(kind, bx, by, core, length, width, i)
+                    pltpu.make_async_copy(g.at[0, :, pl.ds(mine, width)], l.at[slot, block], load_sem.at[bank, slot]).start()
+
+        return carry
+
+    lax.fori_loop(0, chunks + AHEAD + LAG_TWO, body, 0)
+
+    for copy in small:
+        copy.wait()
+    square = jnp.sum(sqa[...], axis=0, keepdims=True) + jnp.sum(sqm[...], axis=0, keepdims=True)
+    for src, received, out in ((gw, rw, ow), (gv, rv, ov)):
+        width = received.shape[2]
+        mean = src[0, :, pl.ds(pl.multiple_of(me * width, width), width)].astype(jnp.float32)
+        for step in range(1, devices):
+            mean = mean + received[step].astype(jnp.float32)
+        mean = mean * (1.0 / devices)
+        out[...] = mean
+        for at in range(0, width, 128):
+            part = mean[:, at:at + 128]
+            square = square + jnp.sum(part * part, axis=0, keepdims=True)
+    tiles[me] = jnp.broadcast_to(square, tiles.shape[1:])
+    share_tile(me, devices, tiles, tsend_sem, trecv_sem)
+    everything = tiles[0]
+    for device in range(1, devices):
+        everything = everything + tiles[device]
+    total[...] = jnp.broadcast_to(jnp.sum(everything[0:1], axis=1, keepdims=True), total.shape)
+
+    def drain(i, carry):
+        chunk = chunks - SLOTS + i
+        slot = lax.rem(chunk, SLOTS)
+        for bank in range(2):
+            out_copy(chunk, slot, bank).wait()
+        return carry
+
+    lax.fori_loop(0, SLOTS, drain, 0)
+
+
+def reduce_scatter(devices, ga, gm, gw, gv):
+    f32, bf16 = jnp.float32, jnp.bfloat16
+    rows = (ga.shape[1], gm.shape[1])
+    lengths = (ga.shape[2] // devices, gm.shape[2] // devices)
+    chunks = lengths[0] // ATTN_WIDTH
+    widths = (ATTN_WIDTH, lengths[1] // chunks)
+    small = (gw.shape[2] // devices, gv.shape[2] // devices)
+
+    def buffers(blocks, dtype):
+        lead = (SLOTS,) if blocks == 1 else (SLOTS, blocks)
+        return [pltpu.VMEM(lead + (rows[bank], widths[bank]), dtype) for bank in range(2)]
+
+    dma = pltpu.SemaphoreType.DMA
+    scratch = (
+        buffers(4, bf16) + buffers(4, bf16) + buffers(2, f32) + buffers(2, f32) + buffers(1, f32) + buffers(1, f32) + buffers(1, f32)
+        + [pltpu.VMEM((devices, gw.shape[1], small[0]), bf16), pltpu.VMEM((devices, gv.shape[1], small[1]), bf16)]
+        + [pltpu.VMEM((rows[bank], 128), f32) for bank in range(2)] + [pltpu.VMEM((devices, 8, 128), f32)]
+        + [dma((2, SLOTS))] * 8 + [dma((devices,))] * 6
+        + [pltpu.SemaphoreType.REGULAR, pltpu.SemaphoreType.REGULAR((2,)), pltpu.SemaphoreType.REGULAR((2,))]
+    )
+    vmem = pl.BlockSpec(memory_space=pltpu.VMEM)
+    anywhere = pl.BlockSpec(memory_space=pl.ANY)
+    return pl.pallas_call(
+        functools.partial(scatter_kernel, devices, widths, chunks),
+        name="scatter",
+        out_shape=[jax.ShapeDtypeStruct((rows[0], lengths[0]), f32), jax.ShapeDtypeStruct((rows[1], lengths[1]), f32),
+                   jax.ShapeDtypeStruct((gw.shape[1], small[0]), f32), jax.ShapeDtypeStruct((gv.shape[1], small[1]), f32),
+                   jax.ShapeDtypeStruct((8, 128), f32)],
+        in_specs=[anywhere, anywhere, vmem, vmem],
+        out_specs=[anywhere, anywhere, vmem, vmem, vmem],
+        scratch_shapes=scratch,
+        compiler_params=pltpu.CompilerParams(collective_id=0, has_side_effects=True, vmem_limit_bytes=48 * 1024 * 1024),
+    )(ga, gm, gw, gv)
+
+
+def share_kernel(devices, part, total, tiles, send_sem, recv_sem):
+    me = lax.axis_index("data")
+    signal_all_and_wait(me, devices)
+    tiles[me] = part[...]
+    share_tile(me, devices, tiles, send_sem, recv_sem)
+    everything = tiles[0]
+    for device in range(1, devices):
+        everything = everything + tiles[device]
+    total[...] = everything
+
+
+def sum_over_devices(devices, part):
+    dma = pltpu.SemaphoreType.DMA
+    vmem = pl.BlockSpec(memory_space=pltpu.VMEM)
+    return pl.pallas_call(
+        functools.partial(share_kernel, devices),
+        name="share",
+        out_shape=jax.ShapeDtypeStruct(part.shape, part.dtype),
+        in_specs=[vmem],
+        out_specs=vmem,
+        scratch_shapes=[pltpu.VMEM((devices,) + part.shape, part.dtype), dma((devices,)), dma((devices,))],
+        compiler_params=pltpu.CompilerParams(collective_id=1, has_side_effects=True),
+    )(part)
+
 
 def adam_direction(mean_grad, weight, first_moment, second_moment, clip_coef):
     clipped = clip_coef * mean_grad
@@ -27,22 +306,16 @@
     full_spec = P(None, None)
 
     def local_step(*all_banks):
-        grad_banks = all_banks[0:4]
         weights = all_banks[4:8]
         firsts = all_banks[8:12]
         seconds = all_banks[12:16]
-        mean_grads = []
-        for grad_bank in grad_banks:
-            row_count = grad_bank.shape[1]
-            shard_width = grad_bank.shape[2] // group_size
-            by_owner = grad_bank.reshape(row_count, group_size, shard_width)
-            received = lax.all_to_all(by_owner, "data", 1, 1, tiled=True)
-            mean_grads.append(jnp.sum(received, axis=1, dtype=jnp.float32) / group_size)
-        local_square = sum(jnp.sum(mean_grad * mean_grad) for mean_grad in mean_grads)
-        clip_coef = jnp.minimum(1.0, MAX_NORM / jnp.sqrt(lax.psum(local_square, "data")))
+        *mean_grads, total_square = reduce_scatter(group_size, *all_banks[0:4])
+        clip_coef = jnp.minimum(1.0, MAX_NORM / jnp.sqrt(total_square[0, 0]))
         results = [adam_direction(mean_grads[bank_index], weights[bank_index], firsts[bank_index], seconds[bank_index], clip_coef) for bank_index in range(4)]
         part_sums = jnp.concatenate([jnp.sum(weight * weight, axis=1) for weight in weights] + [jnp.sum(result[0] * result[0], axis=1) for result in results])
-        norm_sums = lax.psum(part_sums, "data")
+        count = part_sums.shape[0]
+        tile = jnp.pad(part_sums, (0, 1024 - count)).reshape(8, 128)
+        norm_sums = sum_over_devices(group_size, tile).reshape(1024)[:count]
         tensor_count = norm_sums.shape[0] // 2
         trust_ratios = jnp.sqrt(norm_sums[:tensor_count]) / jnp.sqrt(norm_sums[tensor_count:])
         replicas, new_weights = [], []

time: 1900 us -> 1440 us (0.76)
  Pallas kernels: 0 us -> 828 us
  waiting for transfers between devices: 1110 us -> 406 us
  blocking collectives: 444 us -> 23.2 us
  local copies, waits for them, and re-layouts: 151 us -> 71.2 us
  other arithmetic: 160 us -> 96.5 us
    pallas_call x0 -> x2, Pallas kernels: none -> 828 us  [the longest x1 822 us: reduce_scatter(): pl.pallas_call(functools.partial(scatter_kernel, devices, widths, chunks)...]
    all_to_all x3 -> x0, waiting for transfers between devices: 704 us -> none  [local_step(): received = lax.all_to_all(by_owner, 'data', 1, 1, tiled=True)]
    all_to_all x1 -> x0, blocking collectives: 373 us -> none  [local_step(): received = lax.all_to_all(by_owner, 'data', 1, 1, tiled=True)]
    reduce_sum x8 -> x0, other arithmetic: 64.1 us -> none  [the longest x4 51.8 us: local_step(): mean_grads.append(jnp.sum(received, axis=1, dtype=jnp.float32) / group_size)]
    psum x2 -> x0, blocking collectives: 45.6 us -> none  [the longest x1 23.2 us: local_step(): norm_sums = lax.psum(part_sums, 'data')]
    reshape x4 -> x1, local copies, waits for them, and re-layouts: 45.9 us -> 0.6 us  [local_step(): tile = jnp.pad(part_sums, (0, 1024 - count)).reshape(8, 128)]
    unnamed x24, local copies, waits for them, and re-layouts: 105 us -> 70 us
  transfers between devices with their start and end apart: 5 -> 2, of which waited for: 4 -> 2; matrix products, arithmetic and copies ran while one was open for 7% -> 2% of each run, Pallas kernels for 0% -> 0%
where the time goes in v1:
time: 1440 us
  Pallas kernels  828 us (58%)
  waiting for transfers between devices  406 us (28%)
  other arithmetic  96.5 us (7%)
  local copies, waits for them, and re-layouts  71.2 us (5%)
  blocking collectives  23.2 us (2%)
  between operations  14.9 us (1%)
    pallas_call x1, Pallas kernels, reduce_scatter(): pl.pallas_call(functools.partial(scatter_kernel, devices, widths, chunks)...  822 us
    all_gather x2, waiting for transfers between devices, local_step(): lax.all_gather(new_weight.astype(jnp.bfloat16), 'data', axis=1, tiled=True)  406 us
    unnamed x24, local copies, waits for them, and re-layouts  70 us
    reduce_sum x4, other arithmetic, local_step(): jnp.sum(result[0] * result[0], axis=1)  54.6 us
    convert_element_type x4, other arithmetic, local_step(): new_weight.astype(jnp.bfloat16)  40.8 us
  transfers between devices with their start and end apart: 2, of which 2 were waited for; matrix products, arithmetic and copies ran while one was open for 2% of the time, Pallas kernels for 0%

profile of v1, /device:TPU:0, one launch (start us, length us, event | category | flops | bytes accessed | tf_op | source)
XLA Modules:
  0.0 1439.4 jit_solution(17034781110655495723)
XLA Ops:
  7.2 0.0 all-gather.3.cloned.1.call-start
  7.2 0.0 copy-start
  7.2 0.8 copy-done
  8.1 0.0 copy-start.1
  8.1 0.8 copy-done.1
  8.8 0.0 copy-start.8
  8.8 0.0 copy-start.9
  8.8 821.8 %scatter.1 = (f32[12,131072]{1,0:T(8,128)}, f32[6,524288]{1,0:T(8,128)}, f32[3,512]{1,0:T(4,128)S(1)}, f32[29,128]{1,0:T(8,128)S(1)}, f32[8,128]{1,0:T(8,128)S(1)}) custom-call(bf16[1,12,1048576]{2,1,0:T(8,128)(2,1)} %ga.1, bf16[1,6,4194304]{2,1,0:T(8,128)(2,1)} %gm.1, bf16[1,3,4096]{2,1,0:T(4,128)(2,1)S(1)} %copy-done.1, bf16[1,29,1024]{2,1,0:T(8,128)(2,1)S(1)} %copy-done), custom_call_target="tpu_custom_call" | custom-call | tf_op jit(solution)/shard_map/scatter/pallas_call | solution.py:256
  830.7 0.5 slice.24
  831.9 0.0 copy-done.5
  831.9 0.0 copy-done.8
  831.9 0.0 copy-done.9
  831.9 0.8 multiply_reduce_fusion.6
  832.7 0.0 copy-start.2
  832.7 0.0 copy-start.6
  832.7 0.0 copy-start.7
  832.7 33.5 %multiply_reduce_fusion = (f32[6]{0:T(128)S(1)}, f32[6]{0:T(128)S(1)}, f32[6,524288]{1,0:T(8,128)}, f32[6,524288]{1,0:T(8,128)}) fusion(f32[6,524288]{1,0:T(8,128)} %param.21, f32[6,524288]{1,0:T(8,128)} %get-tuple-element.23, f32[]{:T(128)} %bitcast, f32[6,524288]{1,0:T(8,128)} %param.25, f32[6,524288]{1,0:T(8,128)} %param.29), kind=kLoop, calls=%fused_computation.1 | loop fusion | flops 56623088 | bytes 75497520 | tf_op jit(solution)/shard_map/reduce_sum | solution.py:315
  866.2 0.0 copy-done.2
  866.2 0.0 copy-done.6
  866.2 0.0 copy-done.7
  866.2 0.1 multiply_reduce_fusion.4
  866.4 0.0 copy-start.3
  866.4 0.0 copy-start.4
  866.4 20.2 %multiply_reduce_fusion.2 = (f32[12]{0:T(128)S(1)}, f32[12]{0:T(128)S(1)}, f32[12,131072]{1,0:T(8,128)}, f32[12,131072]{1,0:T(8,128)}) fusion(f32[12,131072]{1,0:T(8,128)} %param.20, f32[12,131072]{1,0:T(8,128)} %get-tuple-element.22, f32[]{:T(128)} %bitcast, f32[12,131072]{1,0:T(8,128)} %param.24, f32[12,131072]{1,0:T(8,128)} %param.28), kind=kLoop, calls=%fused_computation.7 | loop fusion | flops 28311528 | bytes 37748836 | tf_op jit(solution)/shard_map/reduce_sum | solution.py:315
  886.6 0.1 concatenate.3
  886.7 0.6 pad_bitcast_fusion.part
  887.3 5.9 share.1
  893.2 0.8 rsqrt_multiply_fusion
  894.0 14.0 fusion.3
  908.0 0.0 all-gather.3.cloned.1.call-update
  908.0 0.2 all-gather.5.cloned.1.call-start
  908.3 0.1 slice_multiply_fusion.2
  908.3 25.5 %fusion.2 = (bf16[6,524288]{1,0:T(8,128)(2,1)}, f32[6,524288]{1,0:T(8,128)}) fusion(f32[6,524288]{1,0:T(8,128)} %param.21, f32[6,524288]{1,0:T(8,128)} %get-tuple-element.80, f32[6,524288]{1,0:T(8,128)} %get-tuple-element.76, f32[6]{0:T(128)S(1)} %slice_multiply_fusion.2), kind=kLoop, calls=%fused_computation.32 | loop fusion | flops 28311552 | bytes 56623128 | tf_op jit(solution)/shard_map/convert_element_type | solution.py:329
  933.9 0.0 all-gather.5.cloned.1.call-update
  933.9 0.1 slice_multiply_fusion
  934.0 0.0 copy-done.3
  934.0 0.0 copy-done.4
  934.0 0.7 fusion
  934.6 11.5 all_gather.15
  946.2 0.1 slice_multiply_fusion.1
  946.3 0.7 fusion.1
  946.9 11.6 all_gather.14
  958.6 106.0 %all-gather.3.cloned.1.call-done = bf16[12,1048576]{1,0:T(8,128)(2,1)} async-done(((bf16[12,131072]{1,0:T(8,128)(2,1)}), bf16[12,1048576]{1,0:T(8,128)(2,1)}) %all-gather.3.cloned.1.call-update) | async-done | bytes 25165840 | tf_op jit(solution)/shard_map/all_gather | solution.py:329
  1064.6 299.6 %all-gather.5.cloned.1.call-done = bf16[6,4194304]{1,0:T(8,128)(2,1)} async-done(((bf16[6,524288]{1,0:T(8,128)(2,1)}), bf16[6,4194304]{1,0:T(8,128)(2,1)}) %all-gather.5.cloned.1.call-update) | async-done | bytes 50331664 | tf_op jit(solution)/shard_map/all_gather | solution.py:329
  1364.2 22.9 %copy.36 = bf16[12,1048576]{1,0:T(8,128)(2,1)} copy(bf16[12,1048576]{1,0:T(8,128)(2,1)} %all-gather.3.cloned.1.call-done) | data formatting | bytes 50331648
  1387.0 44.3 %copy.37 = bf16[6,4194304]{1,0:T(8,128)(2,1)} copy(bf16[6,4194304]{1,0:T(8,128)(2,1)} %all-gather.5.cloned.1.call-done) | data formatting | bytes 100663296
  1431.3 0.6 copy.38
  1431.9 0.6 copy.39
  (2 shorter events, 0.0 us)
Async XLA Ops:
  7.2 1057.4 %all-gather.3.cloned.1.call-start = ((), (), s32[]{:S(2)}) async-start(), calls=%async_computation | async-start | bytes 37748736 | tf_op jit(solution)/shard_map/all_gather | solution.py:329
  7.2 0.8 copy-start
  8.1 0.8 copy-start.1
  8.8 823.0 %copy-start.5 = (f32[3,512]{1,0:T(4,128)S(1)}, f32[3,512]{1,0:T(4,128)}, u32[]{:S(2)}) copy-start(f32[3,512]{1,0:T(4,128)} %param.22) | copy-start | bytes 18436
  8.8 823.0 %copy-start.8 = (f32[3,512]{1,0:T(4,128)S(1)}, f32[3,512]{1,0:T(4,128)}, u32[]{:S(2)}) copy-start(f32[3,512]{1,0:T(4,128)} %param.26) | copy-start | bytes 18436
  8.8 823.1 %copy-start.9 = (f32[3,512]{1,0:T(4,128)S(1)}, f32[3,512]{1,0:T(4,128)}, u32[]{:S(2)}) copy-start(f32[3,512]{1,0:T(4,128)} %param.30) | copy-start | bytes 18436
  832.7 33.5 %copy-start.2 = (f32[29,128]{1,0:T(8,128)S(1)}, f32[29,128]{1,0:T(8,128)}, u32[]{:S(2)}) copy-start(f32[29,128]{1,0:T(8,128)} %param.23) | copy-start | bytes 44548
  832.7 33.5 %copy-start.6 = (f32[29,128]{1,0:T(8,128)S(1)}, f32[29,128]{1,0:T(8,128)}, u32[]{:S(2)}) copy-start(f32[29,128]{1,0:T(8,128)} %param.27) | copy-start | bytes 44548
  832.7 33.5 %copy-start.7 = (f32[29,128]{1,0:T(8,128)S(1)}, f32[29,128]{1,0:T(8,128)}, u32[]{:S(2)}) copy-start(f32[29,128]{1,0:T(8,128)} %param.31) | copy-start | bytes 44548
  866.4 67.6 %copy-start.3 = (f32[29,128]{1,0:T(8,128)}, f32[29,128]{1,0:T(8,128)S(1)}, u32[]{:S(2)}) copy-start(f32[29,128]{1,0:T(8,128)S(1)} %get-tuple-element.78) | copy-start | bytes 44548
  866.4 67.6 %copy-start.4 = (f32[29,128]{1,0:T(8,128)}, f32[29,128]{1,0:T(8,128)S(1)}, u32[]{:S(2)}) copy-start(f32[29,128]{1,0:T(8,128)S(1)} %get-tuple-element.82) | copy-start | bytes 44548
  908.0 456.2 %all-gather.5.cloned.1.call-start = ((), (), s32[]{:S(2)}) async-start(), calls=%async_computation.1 | async-start | bytes 75497472 | tf_op jit(solution)/shard_map/all_gather | solution.py:329
Sparse Core Ops, SparseCore 0:
  908.1 156.3 all-gather.2
  1066.9 297.1 all-gather.4

commit v2 on v1

--- a/solution.py
+++ b/solution.py
@@ -20,7 +20,8 @@
 AHEAD = 2
 LAG_ONE = 4
 LAG_TWO = 8
-ATTN_WIDTH = 1024
+WIDTH = 1024
+OUT_SLOTS = 4
 
 
 def signal_all_and_wait(me, devices):
@@ -43,9 +44,23 @@
         copy.wait()
 
 
-def scatter_kernel(devices, widths, chunks, ga, gm, gw, gv, oa, om, ow, ov, total,
-                   la, lm, pa, pm, s1a, s1m, r1a, r1m, s2a, s2m, r2a, r2m, ba, bm, rw, rv, sqa, sqm, tiles,
-                   load_sem, psend_sem, precv_sem, send1_sem, recv1_sem, send2_sem, recv2_sem, out_sem,
+def pieces(width):
+    half, wide = width // 2, 4 * width
+    first = width + half
+    return (
+        (0, (0, 8), (0, width), (0, 8), (0, width)),
+        (0, (8, 12), (0, half), (0, 4), (width, first)),
+        (0, (8, 12), (half, width), (4, 8), (width, first)),
+        (1, (0, 6), (0, 3 * width), (0, 6), (first, first + 3 * width)),
+        (1, (0, 2), (3 * width, wide), (6, 8), (first, first + width)),
+        (1, (2, 4), (3 * width, wide), (6, 8), (first + width, first + 2 * width)),
+        (1, (4, 6), (3 * width, wide), (6, 8), (first + 2 * width, first + 3 * width)),
+    )
+
+
+def scatter_kernel(devices, width, chunks, ga, gm, gw, gv, oa, om, ow, ov, total,
+                   la, lm, pa, pm, s1, r1, s2, r2, staged, ua, um, rw, rv, sq, tiles,
+                   load_sem, psend_sem, precv_sem, out_sem, send1_sem, recv1_sem, send2_sem, recv2_sem,
                    wsend_sem, wrecv_sem, vsend_sem, vrecv_sem, tsend_sem, trecv_sem, pcredit, credit1, credit2):
     me = lax.axis_index("data")
     core = lax.rem(me, 2)
@@ -54,7 +69,7 @@
     partner = me + 1 - 2 * core
     xn = y * 4 + (1 - x) * 2 + core
     yn = (1 - y) * 4 + x * 2 + core
-    banks = ((ga, oa, la, pa, s1a, r1a, s2a, r2a, ba, sqa, widths[0]), (gm, om, lm, pm, s1m, r1m, s2m, r2m, bm, sqm, widths[1]))
+    banks = ((ga, oa, la, pa, ua, width), (gm, om, lm, pm, um, 4 * width))
 
     signal_all_and_wait(me, devices)
 
@@ -62,19 +77,14 @@
     for step in range(1, devices):
         other = lax.rem(me + step, devices)
         for src, dst, ssem, rsem in ((gw, rw, wsend_sem, wrecv_sem), (gv, rv, vsend_sem, vrecv_sem)):
-            width = dst.shape[2]
+            small_width = dst.shape[2]
             copy = pltpu.make_async_remote_copy(
-                src_ref=src.at[0, :, pl.ds(pl.multiple_of(other * width, width), width)], dst_ref=dst.at[step],
+                src_ref=src.at[0, :, pl.ds(pl.multiple_of(other * small_width, small_width), small_width)], dst_ref=dst.at[step],
                 send_sem=ssem.at[step], recv_sem=rsem.at[step], device_id=(other,), device_id_type=MESH)
             copy.start()
             small.append(copy)
 
-    sqa[...] = jnp.zeros_like(sqa)
-    sqm[...] = jnp.zeros_like(sqm)
-
-    def column(kind, chip_x, chip_y, owner_core, bank_length, width, chunk):
-        owner = chip_y * 4 + chip_x * 2 + owner_core
-        return pl.multiple_of(owner * bank_length + chunk * width, width)
+    sq[...] = jnp.zeros_like(sq)
 
     def chips(kind):
         fx, fy = x + kind * (1 - 2 * x), y + (1 - kind) * (1 - 2 * y)
@@ -87,21 +97,23 @@
     def second_peer(kind):
         return yn + kind * (xn - yn)
 
-    def send_one(slot, kind, bank):
-        s1, r1 = banks[bank][4], banks[bank][5]
+    def send_one(slot, kind):
         return pltpu.make_async_remote_copy(
-            src_ref=s1.at[slot], dst_ref=r1.at[slot], send_sem=send1_sem.at[bank, slot], recv_sem=recv1_sem.at[bank, slot],
+            src_ref=s1.at[slot], dst_ref=r1.at[slot], send_sem=send1_sem.at[slot], recv_sem=recv1_sem.at[slot],
             device_id=(first_peer(kind),), device_id_type=MESH)
 
-    def send_two(slot, kind, bank):
-        s2, r2 = banks[bank][6], banks[bank][7]
+    def send_two(slot, kind):
         return pltpu.make_async_remote_copy(
-            src_ref=s2.at[slot], dst_ref=r2.at[slot], send_sem=send2_sem.at[bank, slot], recv_sem=recv2_sem.at[bank, slot],
+            src_ref=s2.at[slot], dst_ref=r2.at[slot], send_sem=send2_sem.at[slot], recv_sem=recv2_sem.at[slot],
             device_id=(second_peer(kind),), device_id_type=MESH)
 
-    def out_copy(chunk, slot, bank):
-        out, staged, width = banks[bank][1], banks[bank][8], banks[bank][10]
-        return pltpu.make_async_copy(staged.at[slot], out.at[:, pl.ds(pl.multiple_of(chunk * width, width), width)], out_sem.at[bank, slot])
+    def out_copy(chunk, bank):
+        out, unpacked, columns = banks[bank][1], banks[bank][4], banks[bank][5]
+        slot = lax.rem(chunk, OUT_SLOTS)
+        return pltpu.make_async_copy(unpacked.at[slot], out.at[:, pl.ds(pl.multiple_of(chunk * columns, columns), columns)], out_sem.at[bank, slot])
+
+    def pair_sums(slot, block):
+        return [banks[bank][2][slot, block].astype(jnp.float32) + banks[bank][3][slot, block].astype(jnp.float32) for bank in range(2)]
 
     def body(i, carry):
         d = i - AHEAD - LAG_TWO
@@ -110,23 +122,31 @@
         def _():
             slot = lax.rem(d, SLOTS)
             kind = lax.rem(d, 2)
+            send_two(slot, kind).wait_recv()
+
+            @pl.when(d >= OUT_SLOTS)
+            def _():
+                for bank in range(2):
+                    out_copy(d - OUT_SLOTS, bank).wait()
+
+            square = sq[...]
+            for at in range(0, s2.shape[2], 128):
+                mean = (staged[slot, :, at:at + 128] + r2[slot, :, at:at + 128]) * (1.0 / devices)
+                staged[slot, :, at:at + 128] = mean
+                square = square + mean * mean
+            sq[...] = square
+            out_slot = lax.rem(d, OUT_SLOTS)
+            for bank, rows, columns, packed_rows, packed_columns in pieces(width):
+                banks[bank][4][out_slot, rows[0]:rows[1], columns[0]:columns[1]] = staged[slot, packed_rows[0]:packed_rows[1], packed_columns[0]:packed_columns[1]]
             for bank in range(2):
-                r2, staged, sq, width = banks[bank][7], banks[bank][8], banks[bank][9], banks[bank][10]
-                one, two = send_one(slot, kind, bank), send_two(slot, kind, bank)
-                two.wait_recv()
-                one.wait_send()
-                two.wait_send()
-                square = sq[...]
-                for at in range(0, width, 128):
-                    mean = (staged[slot, :, at:at + 128] + r2[slot, :, at:at + 128]) * (1.0 / devices)
-                    staged[slot, :, at:at + 128] = mean
-                    square = square + mean * mean
-                sq[...] = square
-                out_copy(d, slot, bank).start()
+                out_copy(d, bank).start()
 
             @pl.when(d + SLOTS < chunks)
             def _():
                 pl.semaphore_signal(credit2.at[kind], inc=1, device_id=(second_peer(kind),), device_id_type=MESH)
+
+            send_one(slot, kind).wait_send()
+            send_two(slot, kind).wait_send()
 
         c = i - AHEAD - LAG_ONE
 
@@ -139,23 +159,25 @@
             def _():
                 pl.semaphore_wait(credit2.at[kind], 1)
 
-            for bank in range(2):
-                l, p, r1, s2, staged = banks[bank][2], banks[bank][3], banks[bank][5], banks[bank][6], banks[bank][8]
-                send_one(slot, kind, bank).wait_recv()
-                pltpu.make_async_copy(p.at[slot], p.at[slot], psend_sem.at[bank, slot]).wait()
-
-                @pl.when(c >= SLOTS)
-                def _():
-                    out_copy(c - SLOTS, slot, bank).wait()
-
-                s2[slot] = r1[slot, 1] + (l[slot, 1].astype(jnp.float32) + p[slot, 1].astype(jnp.float32))
-                send_two(slot, kind, bank).start()
-                staged[slot] = r1[slot, 0] + (l[slot, 0].astype(jnp.float32) + p[slot, 0].astype(jnp.float32))
+            send_one(slot, kind).wait_recv()
+            sums = pair_sums(slot, 1)
+            for bank, rows, columns, packed_rows, packed_columns in pieces(width):
+                at = (slice(*packed_rows), slice(*packed_columns))
+                s2[(slot, *at)] = r1[(slot, 1, *at)] + sums[bank][rows[0]:rows[1], columns[0]:columns[1]]
+            send_two(slot, kind).start()
+            sums = pair_sums(slot, 0)
+            for bank, rows, columns, packed_rows, packed_columns in pieces(width):
+                at = (slice(*packed_rows), slice(*packed_columns))
+                staged[(slot, *at)] = r1[(slot, 0, *at)] + sums[bank][rows[0]:rows[1], columns[0]:columns[1]]
 
             @pl.when(c + SLOTS < chunks)
             def _():
                 pl.semaphore_signal(pcredit, inc=1, device_id=(partner,), device_id_type=MESH)
                 pl.semaphore_signal(credit1.at[kind], inc=1, device_id=(first_peer(kind),), device_id_type=MESH)
+
+            for bank in range(2):
+                p = banks[bank][3]
+                pltpu.make_async_copy(p.at[slot], p.at[slot], psend_sem.at[bank, slot]).wait()
 
         b = i - AHEAD
 
@@ -169,12 +191,14 @@
                 pl.semaphore_wait(credit1.at[kind], 1)
 
             for bank in range(2):
-                l, p, s1 = banks[bank][2], banks[bank][3], banks[bank][4]
+                l, p = banks[bank][2], banks[bank][3]
                 pltpu.make_async_copy(l.at[slot], l.at[slot], load_sem.at[bank, slot]).wait()
                 pltpu.make_async_copy(p.at[slot], p.at[slot], precv_sem.at[bank, slot]).wait()
-                for block in range(2):
-                    s1[slot, block] = l[slot, 2 + block].astype(jnp.float32) + p[slot, 2 + block].astype(jnp.float32)
-                send_one(slot, kind, bank).start()
+            for block in range(2):
+                sums = pair_sums(slot, 2 + block)
+                for bank, rows, columns, packed_rows, packed_columns in pieces(width):
+                    s1[slot, block, packed_rows[0]:packed_rows[1], packed_columns[0]:packed_columns[1]] = sums[bank][rows[0]:rows[1], columns[0]:columns[1]]
+            send_one(slot, kind).start()
 
         @pl.when(i < chunks)
         def _():
@@ -186,16 +210,17 @@
                 pl.semaphore_wait(pcredit, 1)
 
             for bank in range(2):
-                g, l, p, width = banks[bank][0], banks[bank][2], banks[bank][3], banks[bank][10]
+                g, l, p, columns = banks[bank][0], banks[bank][2], banks[bank][3], banks[bank][5]
                 length = g.shape[2] // devices
                 for block, (bx, by) in enumerate(chips(kind)):
-                    theirs = column(kind, bx, by, 1 - core, length, width, i)
+                    chip = by * 4 + bx * 2
+                    theirs = pl.multiple_of((chip + 1 - core) * length + i * columns, columns)
                     pltpu.make_async_remote_copy(
-                        src_ref=g.at[0, :, pl.ds(theirs, width)], dst_ref=p.at[slot, block],
+                        src_ref=g.at[0, :, pl.ds(theirs, columns)], dst_ref=p.at[slot, block],
                         send_sem=psend_sem.at[bank, slot], recv_sem=precv_sem.at[bank, slot],
                         device_id=(partner,), device_id_type=MESH).start()
-                    mine = column(kind, bx, by, core, length, width, i)
-                    pltpu.make_async_copy(g.at[0, :, pl.ds(mine, width)], l.at[slot, block], load_sem.at[bank, slot]).start()
+                    mine = pl.multiple_of((chip + core) * length + i * columns, columns)
+                    pltpu.make_async_copy(g.at[0, :, pl.ds(mine, columns)], l.at[slot, block], load_sem.at[bank, slot]).start()
 
         return carry
 
@@ -203,15 +228,15 @@
 
     for copy in small:
         copy.wait()
-    square = jnp.sum(sqa[...], axis=0, keepdims=True) + jnp.sum(sqm[...], axis=0, keepdims=True)
+    square = jnp.sum(sq[...], axis=0, keepdims=True)
     for src, received, out in ((gw, rw, ow), (gv, rv, ov)):
-        width = received.shape[2]
-        mean = src[0, :, pl.ds(pl.multiple_of(me * width, width), width)].astype(jnp.float32)
+        small_width = received.shape[2]
+        mean = src[0, :, pl.ds(pl.multiple_of(me * small_width, small_width), small_width)].astype(jnp.float32)
         for step in range(1, devices):
             mean = mean + received[step].astype(jnp.float32)
         mean = mean * (1.0 / devices)
         out[...] = mean
-        for at in range(0, width, 128):
+        for at in range(0, small_width, 128):
             part = mean[:, at:at + 128]
             square = square + jnp.sum(part * part, axis=0, keepdims=True)
     tiles[me] = jnp.broadcast_to(square, tiles.shape[1:])
@@ -221,40 +246,37 @@
         everything = everything + tiles[device]
     total[...] = jnp.broadcast_to(jnp.sum(everything[0:1], axis=1, keepdims=True), total.shape)
 
-    def drain(i, carry):
-        chunk = chunks - SLOTS + i
-        slot = lax.rem(chunk, SLOTS)
+    for chunk in range(chunks - OUT_SLOTS, chunks):
         for bank in range(2):
-            out_copy(chunk, slot, bank).wait()
-        return carry
-
-    lax.fori_loop(0, SLOTS, drain, 0)
+            out_copy(chunk, bank).wait()
 
 
 def reduce_scatter(devices, ga, gm, gw, gv):
     f32, bf16 = jnp.float32, jnp.bfloat16
     rows = (ga.shape[1], gm.shape[1])
     lengths = (ga.shape[2] // devices, gm.shape[2] // devices)
-    chunks = lengths[0] // ATTN_WIDTH
-    widths = (ATTN_WIDTH, lengths[1] // chunks)
+    chunks = lengths[0] // WIDTH
+    widths = (WIDTH, lengths[1] // chunks)
     small = (gw.shape[2] // devices, gv.shape[2] // devices)
-
-    def buffers(blocks, dtype):
-        lead = (SLOTS,) if blocks == 1 else (SLOTS, blocks)
+    packed = (rows[0] * widths[0] + rows[1] * widths[1]) // 8
+
+    def unpacked(lead, dtype):
         return [pltpu.VMEM(lead + (rows[bank], widths[bank]), dtype) for bank in range(2)]
 
     dma = pltpu.SemaphoreType.DMA
     scratch = (
-        buffers(4, bf16) + buffers(4, bf16) + buffers(2, f32) + buffers(2, f32) + buffers(1, f32) + buffers(1, f32) + buffers(1, f32)
+        unpacked((SLOTS, 4), bf16) + unpacked((SLOTS, 4), bf16)
+        + [pltpu.VMEM((SLOTS, 2, 8, packed), f32)] * 2 + [pltpu.VMEM((SLOTS, 8, packed), f32)] * 3
+        + unpacked((OUT_SLOTS,), f32)
         + [pltpu.VMEM((devices, gw.shape[1], small[0]), bf16), pltpu.VMEM((devices, gv.shape[1], small[1]), bf16)]
-        + [pltpu.VMEM((rows[bank], 128), f32) for bank in range(2)] + [pltpu.VMEM((devices, 8, 128), f32)]
-        + [dma((2, SLOTS))] * 8 + [dma((devices,))] * 6
+        + [pltpu.VMEM((8, 128), f32), pltpu.VMEM((devices, 8, 128), f32)]
+        + [dma((2, SLOTS))] * 3 + [dma((2, OUT_SLOTS))] + [dma((SLOTS,))] * 4 + [dma((devices,))] * 6
         + [pltpu.SemaphoreType.REGULAR, pltpu.SemaphoreType.REGULAR((2,)), pltpu.SemaphoreType.REGULAR((2,))]
     )
     vmem = pl.BlockSpec(memory_space=pltpu.VMEM)
     anywhere = pl.BlockSpec(memory_space=pl.ANY)
     return pl.pallas_call(
-        functools.partial(scatter_kernel, devices, widths, chunks),
+        functools.partial(scatter_kernel, devices, WIDTH, chunks),
         name="scatter",
         out_shape=[jax.ShapeDtypeStruct((rows[0], lengths[0]), f32), jax.ShapeDtypeStruct((rows[1], lengths[1]), f32),
                    jax.ShapeDtypeStruct((gw.shape[1], small[0]), f32), jax.ShapeDtypeStruct((gv.shape[1], small[1]), f32),

time: 1440 us -> 1240 us (0.86)
  Pallas kernels: 828 us -> 626 us
    pallas_call x1, Pallas kernels: 822 us -> 620 us  [reduce_scatter(): pl.pallas_call(functools.partial(scatter_kernel, devices, WIDTH, chunks),...]
where the time goes in v2:
time: 1240 us
  Pallas kernels  626 us (50%)
  waiting for transfers between devices  406 us (33%)
  other arithmetic  96.5 us (8%)
  local copies, waits for them, and re-layouts  71.2 us (6%)
  blocking collectives  23.2 us (2%)
  between operations  14.9 us (1%)
    pallas_call x1, Pallas kernels, reduce_scatter(): pl.pallas_call(functools.partial(scatter_kernel, devices, WIDTH, chunks),...  620 us
    all_gather x2, waiting for transfers between devices, local_step(): lax.all_gather(new_weight.astype(jnp.bfloat16), 'data', axis=1, tiled=True)  406 us
    unnamed x24, local copies, waits for them, and re-layouts  70 us
    reduce_sum x4, other arithmetic, local_step(): jnp.sum(result[0] * result[0], axis=1)  54.6 us
    convert_element_type x4, other arithmetic, local_step(): new_weight.astype(jnp.bfloat16)  40.8 us
  transfers between devices with their start and end apart: 2, of which 2 were waited for; matrix products, arithmetic and copies ran while one was open for 2% of the time, Pallas kernels for 0%

profile of v2, /device:TPU:0, one launch (start us, length us, event | category | flops | bytes accessed | tf_op | source)
XLA Modules:
  0.0 1237.2 jit_solution(13548739001164667381)
XLA Ops:
  7.2 0.0 all-gather.3.cloned.1.call-start
  7.2 0.0 copy-start
  7.2 0.8 copy-done
  8.1 0.0 copy-start.1
  8.1 0.8 copy-done.1
  8.8 0.0 copy-start.8
  8.8 0.0 copy-start.9
  8.8 619.5 %scatter.1 = (f32[12,131072]{1,0:T(8,128)}, f32[6,524288]{1,0:T(8,128)}, f32[3,512]{1,0:T(4,128)S(1)}, f32[29,128]{1,0:T(8,128)S(1)}, f32[8,128]{1,0:T(8,128)S(1)}) custom-call(bf16[1,12,1048576]{2,1,0:T(8,128)(2,1)} %ga.1, bf16[1,6,4194304]{2,1,0:T(8,128)(2,1)} %gm.1, bf16[1,3,4096]{2,1,0:T(4,128)(2,1)S(1)} %copy-done.1, bf16[1,29,1024]{2,1,0:T(8,128)(2,1)S(1)} %copy-done), custom_call_target="tpu_custom_call" | custom-call | tf_op jit(solution)/shard_map/scatter/pallas_call | solution.py:278
  628.4 0.5 slice.24
  629.6 0.0 copy-done.5
  629.6 0.0 copy-done.8
  629.6 0.0 copy-done.9
  629.6 0.8 multiply_reduce_fusion.6
  630.3 0.0 copy-start.2
  630.4 0.0 copy-start.6
  630.4 0.0 copy-start.7
  630.4 33.5 %multiply_reduce_fusion = (f32[6]{0:T(128)S(1)}, f32[6]{0:T(128)S(1)}, f32[6,524288]{1,0:T(8,128)}, f32[6,524288]{1,0:T(8,128)}) fusion(f32[6,524288]{1,0:T(8,128)} %param.21, f32[6,524288]{1,0:T(8,128)} %get-tuple-element.23, f32[]{:T(128)} %bitcast, f32[6,524288]{1,0:T(8,128)} %param.25, f32[6,524288]{1,0:T(8,128)} %param.29), kind=kLoop, calls=%fused_computation.1 | loop fusion | flops 56623088 | bytes 75497520 | tf_op jit(solution)/shard_map/reduce_sum | solution.py:337
  663.9 0.0 copy-done.2
  663.9 0.0 copy-done.6
  663.9 0.0 copy-done.7
  663.9 0.1 multiply_reduce_fusion.4
  664.1 0.0 copy-start.3
  664.1 0.0 copy-start.4
  664.1 20.2 %multiply_reduce_fusion.2 = (f32[12]{0:T(128)S(1)}, f32[12]{0:T(128)S(1)}, f32[12,131072]{1,0:T(8,128)}, f32[12,131072]{1,0:T(8,128)}) fusion(f32[12,131072]{1,0:T(8,128)} %param.20, f32[12,131072]{1,0:T(8,128)} %get-tuple-element.22, f32[]{:T(128)} %bitcast, f32[12,131072]{1,0:T(8,128)} %param.24, f32[12,131072]{1,0:T(8,128)} %param.28), kind=kLoop, calls=%fused_computation.7 | loop fusion | flops 28311528 | bytes 37748836 | tf_op jit(solution)/shard_map/reduce_sum | solution.py:337
  684.3 0.1 concatenate.3
  684.3 0.6 pad_bitcast_fusion.part
  684.9 6.0 share.1
  691.0 0.8 rsqrt_multiply_fusion
  691.8 14.0 %fusion.3 = (bf16[12,131072]{1,0:T(8,128)(2,1)}, f32[12,131072]{1,0:T(8,128)}) fusion(f32[12,131072]{1,0:T(8,128)} %param.20, f32[12,131072]{1,0:T(8,128)} %get-tuple-element.79, f32[12,131072]{1,0:T(8,128)} %get-tuple-element.75, f32[12]{0:T(128)S(1)} %slice_multiply_fusion.3), kind=kLoop, calls=%fused_computation.33 | loop fusion | flops 14155776 | bytes 28311600 | tf_op jit(solution)/shard_map/convert_element_type | solution.py:351
  705.8 0.0 all-gather.3.cloned.1.call-update
  705.8 0.2 all-gather.5.cloned.1.call-start
  706.0 0.1 slice_multiply_fusion.2
  706.1 25.5 %fusion.2 = (bf16[6,524288]{1,0:T(8,128)(2,1)}, f32[6,524288]{1,0:T(8,128)}) fusion(f32[6,524288]{1,0:T(8,128)} %param.21, f32[6,524288]{1,0:T(8,128)} %get-tuple-element.80, f32[6,524288]{1,0:T(8,128)} %get-tuple-element.76, f32[6]{0:T(128)S(1)} %slice_multiply_fusion.2), kind=kLoop, calls=%fused_computation.32 | loop fusion | flops 28311552 | bytes 56623128 | tf_op jit(solution)/shard_map/convert_element_type | solution.py:351
  731.6 0.0 all-gather.5.cloned.1.call-update
  731.6 0.1 slice_multiply_fusion
  731.7 0.0 copy-done.3
  731.7 0.0 copy-done.4
  731.7 0.7 fusion
  732.4 11.5 all_gather.15
  744.0 0.1 slice_multiply_fusion.1
  744.0 0.7 fusion.1
  744.7 11.6 all_gather.14
  756.3 106.0 %all-gather.3.cloned.1.call-done = bf16[12,1048576]{1,0:T(8,128)(2,1)} async-done(((bf16[12,131072]{1,0:T(8,128)(2,1)}), bf16[12,1048576]{1,0:T(8,128)(2,1)}) %all-gather.3.cloned.1.call-update) | async-done | bytes 25165840 | tf_op jit(solution)/shard_map/all_gather | solution.py:351
  862.3 299.6 %all-gather.5.cloned.1.call-done = bf16[6,4194304]{1,0:T(8,128)(2,1)} async-done(((bf16[6,524288]{1,0:T(8,128)(2,1)}), bf16[6,4194304]{1,0:T(8,128)(2,1)}) %all-gather.5.cloned.1.call-update) | async-done | bytes 50331664 | tf_op jit(solution)/shard_map/all_gather | solution.py:351
  1162.0 22.9 %copy.36 = bf16[12,1048576]{1,0:T(8,128)(2,1)} copy(bf16[12,1048576]{1,0:T(8,128)(2,1)} %all-gather.3.cloned.1.call-done) | data formatting | bytes 50331648
  1184.8 44.3 %copy.37 = bf16[6,4194304]{1,0:T(8,128)(2,1)} copy(bf16[6,4194304]{1,0:T(8,128)(2,1)} %all-gather.5.cloned.1.call-done) | data formatting | bytes 100663296
  1229.1 0.6 copy.38
  1229.7 0.6 copy.39
  (2 shorter events, 0.0 us)
Async XLA Ops:
  7.2 855.2 %all-gather.3.cloned.1.call-start = ((), (), s32[]{:S(2)}) async-start(), calls=%async_computation | async-start | bytes 37748736 | tf_op jit(solution)/shard_map/all_gather | solution.py:351
  7.2 0.8 copy-start
  8.1 0.8 copy-start.1
  8.8 620.7 %copy-start.5 = (f32[3,512]{1,0:T(4,128)S(1)}, f32[3,512]{1,0:T(4,128)}, u32[]{:S(2)}) copy-start(f32[3,512]{1,0:T(4,128)} %param.22) | copy-start | bytes 18436
  8.8 620.7 %copy-start.8 = (f32[3,512]{1,0:T(4,128)S(1)}, f32[3,512]{1,0:T(4,128)}, u32[]{:S(2)}) copy-start(f32[3,512]{1,0:T(4,128)} %param.26) | copy-start | bytes 18436
  8.8 620.8 %copy-start.9 = (f32[3,512]{1,0:T(4,128)S(1)}, f32[3,512]{1,0:T(4,128)}, u32[]{:S(2)}) copy-start(f32[3,512]{1,0:T(4,128)} %param.30) | copy-start | bytes 18436
  630.3 33.5 %copy-start.2 = (f32[29,128]{1,0:T(8,128)S(1)}, f32[29,128]{1,0:T(8,128)}, u32[]{:S(2)}) copy-start(f32[29,128]{1,0:T(8,128)} %param.23) | copy-start | bytes 44548
  630.4 33.5 %copy-start.6 = (f32[29,128]{1,0:T(8,128)S(1)}, f32[29,128]{1,0:T(8,128)}, u32[]{:S(2)}) copy-start(f32[29,128]{1,0:T(8,128)} %param.27) | copy-start | bytes 44548
  630.4 33.5 %copy-start.7 = (f32[29,128]{1,0:T(8,128)S(1)}, f32[29,128]{1,0:T(8,128)}, u32[]{:S(2)}) copy-start(f32[29,128]{1,0:T(8,128)} %param.31) | copy-start | bytes 44548
  664.1 67.7 %copy-start.3 = (f32[29,128]{1,0:T(8,128)}, f32[29,128]{1,0:T(8,128)S(1)}, u32[]{:S(2)}) copy-start(f32[29,128]{1,0:T(8,128)S(1)} %get-tuple-element.78) | copy-start | bytes 44548
  664.1 67.7 %copy-start.4 = (f32[29,128]{1,0:T(8,128)}, f32[29,128]{1,0:T(8,128)S(1)}, u32[]{:S(2)}) copy-start(f32[29,128]{1,0:T(8,128)S(1)} %get-tuple-element.82) | copy-start | bytes 44548
  705.8 456.2 %all-gather.5.cloned.1.call-start = ((), (), s32[]{:S(2)}) async-start(), calls=%async_computation.1 | async-start | bytes 75497472 | tf_op jit(solution)/shard_map/all_gather | solution.py:351
Sparse Core Ops, SparseCore 0:
  705.9 156.3 all-gather.2
  864.7 297.1 all-gather.4

commit v3 on v2

--- a/solution.py
+++ b/solution.py
@@ -22,6 +22,9 @@
 LAG_TWO = 8
 WIDTH = 1024
 OUT_SLOTS = 4
+ATTN_BLOCK = 8192
+MLP_BLOCK = 16384
+MLP_SPLITS = (12, 10, 6, 4)
 
 
 def signal_all_and_wait(me, devices):
@@ -288,6 +291,14 @@
     )(ga, gm, gw, gv)
 
 
+def adam_direction(mean_grad, weight, first_moment, second_moment, clip_coef):
+    clipped = clip_coef * mean_grad
+    new_first = BETA_FIRST * first_moment + (1.0 - BETA_FIRST) * clipped
+    new_second = BETA_SECOND * second_moment + (1.0 - BETA_SECOND) * (clipped * clipped)
+    update = (new_first / (1.0 - BETA_FIRST ** STEP_NUMBER)) / (jnp.sqrt(new_second / (1.0 - BETA_SECOND ** STEP_NUMBER)) + EPSILON) + WEIGHT_DECAY * weight
+    return update, new_first, new_second
+
+
 def share_kernel(devices, part, total, tiles, send_sem, recv_sem):
     me = lax.axis_index("data")
     signal_all_and_wait(me, devices)
@@ -296,29 +307,187 @@
     everything = tiles[0]
     for device in range(1, devices):
         everything = everything + tiles[device]
-    total[...] = everything
-
-
-def sum_over_devices(devices, part):
+    if total.shape == part.shape:
+        total[...] = everything
+    else:
+        weight_norm = jnp.sqrt(jnp.sum(everything[0:8], axis=1, keepdims=True))
+        update_norm = jnp.sqrt(jnp.sum(everything[8:16], axis=1, keepdims=True))
+        total[...] = jnp.broadcast_to(LEARN_RATE * (weight_norm / update_norm), total.shape)
+
+
+def sum_over_devices(devices, part, name, collective_id, ratio):
     dma = pltpu.SemaphoreType.DMA
     vmem = pl.BlockSpec(memory_space=pltpu.VMEM)
     return pl.pallas_call(
         functools.partial(share_kernel, devices),
-        name="share",
-        out_shape=jax.ShapeDtypeStruct(part.shape, part.dtype),
+        name=name,
+        out_shape=jax.ShapeDtypeStruct((8, 128) if ratio else part.shape, part.dtype),
         in_specs=[vmem],
         out_specs=vmem,
         scratch_shapes=[pltpu.VMEM((devices,) + part.shape, part.dtype), dma((devices,)), dma((devices,))],
-        compiler_params=pltpu.CompilerParams(collective_id=1, has_side_effects=True),
+        compiler_params=pltpu.CompilerParams(collective_id=collective_id, has_side_effects=True),
     )(part)
 
 
-def adam_direction(mean_grad, weight, first_moment, second_moment, clip_coef):
-    clipped = clip_coef * mean_grad
-    new_first = BETA_FIRST * first_moment + (1.0 - BETA_FIRST) * clipped
-    new_second = BETA_SECOND * second_moment + (1.0 - BETA_SECOND) * (clipped * clipped)
-    update = (new_first / (1.0 - BETA_FIRST ** STEP_NUMBER)) / (jnp.sqrt(new_second / (1.0 - BETA_SECOND ** STEP_NUMBER)) + EPSILON) + WEIGHT_DECAY * weight
-    return update, new_first, new_second
+def moment_kernel(valid, g, w, m, v, total, *refs):
+    new_m, new_v, u, norms = refs[-4:]
+    clip = jnp.minimum(1.0, MAX_NORM / jnp.sqrt(total[...]))
+
+    @pl.when(pl.program_id(0) == 0)
+    def _():
+        norms[...] = jnp.zeros_like(norms)
+
+    def step(index, carry):
+        weight_square, update_square = carry
+        for part in range(8):
+            at = pl.ds(pl.multiple_of(index * 1024 + part * 128, 128), 128)
+            weight = w[:, at]
+            update, first, second = adam_direction(g[:, at], weight, m[:, at], v[:, at], clip)
+            new_m[:, at] = first
+            new_v[:, at] = second
+            u[:, at] = update
+            weight_square = weight_square + weight * weight
+            update_square = update_square + update * update
+        return weight_square, update_square
+
+    zero = jnp.zeros((8, 128), jnp.float32)
+    weight_square, update_square = lax.fori_loop(0, g.shape[1] // 1024, step, (zero, zero))
+    row = lax.broadcasted_iota(jnp.int32, (8, 128), 0)
+    norms[0:8] += jnp.where(row < valid, weight_square, 0.0)
+    norms[8:16] += jnp.where(row < valid, update_square, 0.0)
+
+
+def moments(name, row_block, valid, block, g, w, m, v, total, before=()):
+    f32 = jnp.float32
+    rows, length = g.shape
+    columns = pl.BlockSpec((8, block), lambda i: (row_block, i))
+    whole = jax.ShapeDtypeStruct((rows, length), f32)
+    bytes_moved = 8 * length * 4 * 7
+    return pl.pallas_call(
+        functools.partial(moment_kernel, valid),
+        name=name,
+        grid=(length // block,),
+        out_shape=[whole, whole, jax.ShapeDtypeStruct((8, length), f32), jax.ShapeDtypeStruct((16, 128), f32)],
+        in_specs=[columns] * 4 + [pl.BlockSpec((8, 128), lambda i: (0, 0))] + [pl.BlockSpec(memory_space=pl.ANY)] * len(before),
+        out_specs=[columns, columns, pl.BlockSpec((8, block), lambda i: (0, i)), pl.BlockSpec((16, 128), lambda i: (0, 0))],
+        input_output_aliases={5 + index: index for index in range(len(before))},
+        cost_estimate=pl.CostEstimate(flops=bytes_moved, bytes_accessed=bytes_moved, transcendentals=0),
+        compiler_params=pltpu.CompilerParams(dimension_semantics=("arbitrary",)),
+    )(g, w, m, v, total, *before)
+
+
+def pack(kind, full, packed):
+    if kind == 4:
+        half = packed.shape[1]
+        packed[0:4] = full[0:4, 0:half]
+        packed[4:8] = full[0:4, half:]
+    if kind == 6:
+        quarter = packed.shape[1] // 3
+        packed[0:6] = full[0:6, 0:3 * quarter]
+        for part in range(3):
+            packed[6:8, part * quarter:(part + 1) * quarter] = full[2 * part:2 * part + 2, 3 * quarter:]
+
+
+def weight_kernel(kind, splits, w, u, ratio, *refs):
+    count = len(splits) if splits else 1
+    outs = refs[-2 - count:-1]
+    new_w, sent, packed = outs[0], outs[1:], refs[-1]
+    scale = ratio[...]
+
+    def step(index, carry):
+        for part in range(8):
+            at = pl.ds(pl.multiple_of(index * 1024 + part * 128, 128), 128)
+            new_w[:, at] = w[:, at] - scale * u[:, at]
+        return carry
+
+    lax.fori_loop(0, w.shape[1] // 1024, step, 0)
+    if kind == 8:
+        sent[0][...] = new_w[...].astype(jnp.bfloat16)
+        return
+    pack(kind, new_w, packed)
+    if count == 1:
+        sent[0][...] = packed[...].astype(jnp.bfloat16)
+        return
+    start = 0
+    i = pl.program_id(0)
+    for index, size in enumerate(splits):
+        @pl.when(jnp.logical_and(i >= start, i < start + size))
+        def _():
+            sent[index][...] = packed[...].astype(jnp.bfloat16)
+        start += size
+
+
+def new_weights(name, row_block, kind, block, w, u, ratio, splits=None, before=()):
+    rows, length = w.shape
+    columns = pl.BlockSpec((8, block), lambda i: (row_block, i))
+    width = block * kind // 8
+    parts = splits or (length // block,)
+    starts = [sum(parts[:index]) for index in range(len(parts))]
+    bytes_moved = 8 * length * 4 * 4
+    return pl.pallas_call(
+        functools.partial(weight_kernel, kind, splits),
+        name=name,
+        grid=(length // block,),
+        out_shape=[jax.ShapeDtypeStruct((rows, length), jnp.float32)] + [jax.ShapeDtypeStruct((8, width * part), jnp.bfloat16) for part in parts],
+        in_specs=[columns, pl.BlockSpec((8, block), lambda i: (0, i)), pl.BlockSpec((8, 128), lambda i: (0, 0))]
+        + [pl.BlockSpec(memory_space=pl.ANY)] * len(before),
+        out_specs=[columns] + [pl.BlockSpec((8, width), lambda i, start=start, part=part: (0, jnp.clip(i - start, 0, part - 1))) for start, part in zip(starts, parts)],
+        scratch_shapes=[pltpu.VMEM((8, width), jnp.float32)],
+        input_output_aliases={3: 0} if before else {},
+        cost_estimate=pl.CostEstimate(flops=bytes_moved, bytes_accessed=bytes_moved, transcendentals=0),
+        compiler_params=pltpu.CompilerParams(dimension_semantics=("arbitrary",)),
+    )(w, u, ratio, *before)
+
+
+def unpack_attn_kernel(low, high, out):
+    half = high.shape[2]
+    out[0:8] = low[0]
+    rest = high[0].astype(jnp.float32)
+    out[8:12, 0:half] = rest[0:4].astype(jnp.bfloat16)
+    out[8:12, half:] = rest[4:8].astype(jnp.bfloat16)
+
+
+def unpack_attn(low, high, block):
+    devices, _, length = low.shape
+    blocks = length // block
+    bytes_moved = devices * length * 12 * 4
+    return pl.pallas_call(
+        unpack_attn_kernel,
+        name="unpack_attn",
+        grid=(devices, blocks),
+        out_shape=jax.ShapeDtypeStruct((12, devices * length), jnp.bfloat16),
+        in_specs=[pl.BlockSpec((1, 8, block), lambda d, i: (d, 0, i)), pl.BlockSpec((1, 8, block // 2), lambda d, i: (d, 0, i))],
+        out_specs=pl.BlockSpec((12, block), lambda d, i: (0, d * blocks + i)),
+        cost_estimate=pl.CostEstimate(flops=bytes_moved, bytes_accessed=bytes_moved, transcendentals=0),
+        compiler_params=pltpu.CompilerParams(dimension_semantics=("arbitrary", "arbitrary")),
+    )(low, high)
+
+
+def unpack_mlp_kernel(packed, *refs):
+    out = refs[-1]
+    quarter = packed.shape[2] // 3
+    full = packed[0].astype(jnp.float32)
+    out[:, 0:3 * quarter] = full[0:6].astype(jnp.bfloat16)
+    for part in range(3):
+        out[2 * part:2 * part + 2, 3 * quarter:] = full[6:8, part * quarter:(part + 1) * quarter].astype(jnp.bfloat16)
+
+
+def unpack_mlp(packed, block, start, blocks, before):
+    devices = packed.shape[0]
+    width = block * 6 // 8
+    count = packed.shape[2] // width
+    bytes_moved = packed.size * 4
+    return pl.pallas_call(
+        unpack_mlp_kernel,
+        name=f"unpack_mlp_{start}",
+        grid=(devices, count),
+        out_shape=jax.ShapeDtypeStruct((6, devices * blocks * block), jnp.bfloat16),
+        in_specs=[pl.BlockSpec((1, 8, width), lambda d, i: (d, 0, i))] + [pl.BlockSpec(memory_space=pl.ANY)] * len(before),
+        out_specs=pl.BlockSpec((6, block), lambda d, i: (0, d * blocks + start + i)),
+        input_output_aliases={1: 0} if before else {},
+        cost_estimate=pl.CostEstimate(flops=bytes_moved, bytes_accessed=bytes_moved, transcendentals=0),
+        compiler_params=pltpu.CompilerParams(dimension_semantics=("arbitrary", "arbitrary")),
+    )(packed, *before)
 
 
 def solution(mesh):
@@ -331,24 +500,50 @@
         weights = all_banks[4:8]
         firsts = all_banks[8:12]
         seconds = all_banks[12:16]
-        *mean_grads, total_square = reduce_scatter(group_size, *all_banks[0:4])
-        clip_coef = jnp.minimum(1.0, MAX_NORM / jnp.sqrt(total_square[0, 0]))
-        results = [adam_direction(mean_grads[bank_index], weights[bank_index], firsts[bank_index], seconds[bank_index], clip_coef) for bank_index in range(4)]
-        part_sums = jnp.concatenate([jnp.sum(weight * weight, axis=1) for weight in weights] + [jnp.sum(result[0] * result[0], axis=1) for result in results])
+        *mean_grads, total = reduce_scatter(group_size, *all_banks[0:4])
+
+        state = [(mean_grads[bank], weights[bank], firsts[bank], seconds[bank], total) for bank in range(2)]
+        attn_m, attn_v, u, norms = moments("moments_high", 1, 4, ATTN_BLOCK, *state[0])
+        ratio = sum_over_devices(group_size, norms, "share_high", 1, True)
+        attn_w, sent = new_weights("weights_high", 1, 4, ATTN_BLOCK, weights[0], u, ratio)
+        high = lax.all_gather(sent, "data")
+
+        attn_m, attn_v, u, norms = moments("moments_low", 0, 8, ATTN_BLOCK, *state[0], before=(attn_m, attn_v))
+        ratio = sum_over_devices(group_size, norms, "share_low", 2, True)
+        attn_w, sent = new_weights("weights_low", 0, 8, ATTN_BLOCK, weights[0], u, ratio, before=(attn_w,))
+        low = lax.all_gather(sent, "data")
+
+        mlp_m, mlp_v, u, norms = moments("moments_mlp", 0, 6, MLP_BLOCK, *state[1])
+        ratio = sum_over_devices(group_size, norms, "share_mlp", 3, True)
+        mlp_w, *sent = new_weights("weights_mlp", 0, 6, MLP_BLOCK, weights[1], u, ratio, splits=MLP_SPLITS)
+        gathered = [lax.all_gather(part, "data") for part in sent]
+
+        clip_coef = jnp.minimum(1.0, MAX_NORM / jnp.sqrt(total[0, 0]))
+        results = [adam_direction(mean_grads[bank], weights[bank], firsts[bank], seconds[bank], clip_coef) for bank in (2, 3)]
+        part_sums = jnp.concatenate([jnp.sum(weight * weight, axis=1) for weight in weights[2:]] + [jnp.sum(result[0] * result[0], axis=1) for result in results])
         count = part_sums.shape[0]
         tile = jnp.pad(part_sums, (0, 1024 - count)).reshape(8, 128)
-        norm_sums = sum_over_devices(group_size, tile).reshape(1024)[:count]
-        tensor_count = norm_sums.shape[0] // 2
-        trust_ratios = jnp.sqrt(norm_sums[:tensor_count]) / jnp.sqrt(norm_sums[tensor_count:])
-        replicas, new_weights = [], []
+        norm_sums = sum_over_devices(group_size, tile, "share_small", 4, False).reshape(1024)[:count]
+        trust_ratios = jnp.sqrt(norm_sums[:count // 2]) / jnp.sqrt(norm_sums[count // 2:])
+        small_replicas, small_weights = [], []
         first_row = 0
-        for bank_index in range(4):
-            row_count = weights[bank_index].shape[0]
+        for index in range(2):
+            weight = weights[2 + index]
+            row_count = weight.shape[0]
             trust_ratio = trust_ratios[first_row:first_row + row_count]
             first_row = first_row + row_count
-            new_weight = weights[bank_index] - LEARN_RATE * trust_ratio[:, None] * results[bank_index][0]
-            new_weights.append(new_weight)
-            replicas.append(lax.all_gather(new_weight.astype(jnp.bfloat16), "data", axis=1, tiled=True))
-        return tuple(replicas + new_weights + [result[1] for result in results] + [result[2] for result in results])
+            new_weight = weight - LEARN_RATE * trust_ratio[:, None] * results[index][0]
+            small_weights.append(new_weight)
+            small_replicas.append(lax.all_gather(new_weight.astype(jnp.bfloat16), "data", axis=1, tiled=True))
+
+        attn_replica = unpack_attn(low, high, ATTN_BLOCK)
+        blocks = weights[1].shape[1] // MLP_BLOCK
+        mlp_replica = ()
+        start = 0
+        for part, size in zip(gathered, MLP_SPLITS):
+            mlp_replica = (unpack_mlp(part, MLP_BLOCK, start, blocks, mlp_replica),)
+            start += size
+        return (attn_replica, *mlp_replica, *small_replicas, attn_w, mlp_w, *small_weights,
+                attn_m, mlp_m, results[0][1], results[1][1], attn_v, mlp_v, results[0][2], results[1][2])
 
     return jax.shard_map(local_step, mesh=mesh, in_specs=(grad_spec,) * 4 + (shard_spec,) * 12, out_specs=(full_spec,) * 4 + (shard_spec,) * 12, check_vma=False)

time: 1240 us -> 1110 us (0.90)
  Pallas kernels: 626 us -> 1010 us
  waiting for transfers between devices: 406 us -> 41.7 us
  other arithmetic: 96.5 us -> 3.82 us
  local copies, waits for them, and re-layouts: 71.2 us -> 4.68 us
    pallas_call x1 -> x15, Pallas kernels: 6.02 us -> 393 us  [the longest x4 148 us: unpack_mlp(): pl.pallas_call(unpack_mlp_kernel, name=f'unpack_mlp_{start}', grid=(devic...]
    all_gather x2 -> x6, waiting for transfers between devices: 406 us -> 40.1 us  [the longest x4 40 us: local_step(): gathered = [lax.all_gather(part, 'data') for part in sent]]
    unnamed x24 -> x28, local copies, waits for them, and re-layouts: 70 us -> 3.48 us
    reduce_sum x4 -> x1, other arithmetic: 54.6 us -> 0.75 us  [local_step(): jnp.sum(result[0] * result[0], axis=1)]
    convert_element_type x4 -> x2, other arithmetic: 40.8 us -> 1.36 us  [local_step(): new_weight.astype(jnp.bfloat16)]
  transfers between devices with their start and end apart: 2 -> 6, of which waited for: 2 -> 3; matrix products, arithmetic and copies ran while one was open for 2% -> 0% of each run, Pallas kernels for 0% -> 31%
where the time goes in v3:
time: 1110 us; the launch traced here: 1100 us
  Pallas kernels  1010 us (91%)
  waiting for transfers between devices  41.7 us (4%)
  blocking collectives  23.2 us (2%)
  between operations  15 us (1%)
    pallas_call x1, Pallas kernels, reduce_scatter(): pl.pallas_call(functools.partial(scatter_kernel, devices, WIDTH, chunks),...  620 us
    pallas_call x4, Pallas kernels, unpack_mlp(): pl.pallas_call(unpack_mlp_kernel, name=f'unpack_mlp_{start}', grid=(devic...  148 us
    pallas_call x3, Pallas kernels, moments(): pl.pallas_call(functools.partial(moment_kernel, valid), name=name, grid=(...  90.2 us
    pallas_call x1, Pallas kernels, unpack_attn(): pl.pallas_call(unpack_attn_kernel, name='unpack_attn', grid=(devices, blo...  71.3 us
    pallas_call x3, Pallas kernels, new_weights(): pl.pallas_call(functools.partial(weight_kernel, kind, splits), name=name,...  58.3 us
    all_gather x4, waiting for transfers between devices, local_step(): gathered = [lax.all_gather(part, 'data') for part in sent]  40 us
    pallas_call x4, Pallas kernels, sum_over_devices(): pl.pallas_call(functools.partial(share_kernel, devices), name=name, out_s...  25.5 us
    all_gather x2, blocking collectives, local_step(): lax.all_gather(new_weight.astype(jnp.bfloat16), 'data', axis=1, tiled=True)  23.2 us
  transfers between devices with their start and end apart: 6, of which 3 were waited for; matrix products, arithmetic and copies ran while one was open for 0% of the time, Pallas kernels for 31%

profile of v3, /device:TPU:0, one launch (start us, length us, event | category | flops | bytes accessed | tf_op | source)
XLA Modules:
  0.0 1101.1 jit_solution(6637011705577967510)
XLA Ops:
  7.2 0.0 all-gather.15.cloned.1.call-start
  7.2 0.8 copy-done
  8.1 0.8 copy-done.2
  8.8 619.5 %scatter.1 = (f32[12,131072]{1,0:T(8,128)}, f32[6,524288]{1,0:T(8,128)}, f32[3,512]{1,0:T(4,128)S(1)}, f32[29,128]{1,0:T(8,128)S(1)}, f32[8,128]{1,0:T(8,128)S(1)}) custom-call(bf16[1,12,1048576]{2,1,0:T(8,128)(2,1)} %ga.1, bf16[1,6,4194304]{2,1,0:T(8,128)(2,1)} %gm.1, bf16[1,3,4096]{2,1,0:T(4,128)(2,1)S(1)} %copy-done.2, bf16[1,29,1024]{2,1,0:T(8,128)(2,1)S(1)} %copy-done), custom_call_target="tpu_custom_call" | custom-call | tf_op jit(solution)/shard_map/scatter/pallas_call | solution.py:281
  628.4 0.6 copy-done.1
  628.9 17.7 %moments_high.1 = (f32[12,131072]{1,0:T(8,128)}, f32[12,131072]{1,0:T(8,128)}, f32[8,131072]{1,0:T(8,128)}, f32[16,128]{1,0:T(8,128)}) custom-call(f32[12,131072]{1,0:T(8,128)} %get-tuple-element.42.g, f32[12,131072]{1,0:T(8,128)} %w.9, f32[12,131072]{1,0:T(8,128)} %m.4, f32[12,131072]{1,0:T(8,128)} %v.4, f32[8,128]{1,0:T(8,128)} %copy-done.1), custom_call_target="tpu_custom_call" | custom-call | flops 29360128 | bytes 29360128 | tf_op jit(solution)/shard_map/moments_high/pallas_call | solution.py:366
  646.7 6.3 share_high.1.ratio
  653.0 12.1 %weights_high.1 = (f32[12,131072]{1,0:T(8,128)}, bf16[8,65536]{1,0:T(8,128)(2,1)}) custom-call(f32[12,131072]{1,0:T(8,128)} %w.9, f32[8,131072]{1,0:T(8,128)} %get-tuple-element.48.u, f32[8,128]{1,0:T(8,128)} %share_high.1.ratio), custom_call_target="tpu_custom_call" | custom-call | flops 16777216 | bytes 16777216 | tf_op jit(solution)/shard_map/weights_high/pallas_call | solution.py:427
  665.0 0.0 all-gather.15.cloned.1.call-update
  665.1 0.0 all-gather.13.cloned.1.call-start
  665.1 17.8 %moments_low.1 = (f32[12,131072]{1,0:T(8,128)}, f32[12,131072]{1,0:T(8,128)}, f32[8,131072]{1,0:T(8,128)}, f32[16,128]{1,0:T(8,128)}) custom-call(f32[12,131072]{1,0:T(8,128)} %get-tuple-element.42.g, f32[12,131072]{1,0:T(8,128)} %w.9, f32[12,131072]{1,0:T(8,128)} %m.4, f32[12,131072]{1,0:T(8,128)} %v.4, ...), custom_call_target="tpu_custom_call", output_to_operand_aliasing={{0}: (5, {}), {1}: (6, {})} | custom-call | flops 29360128 | bytes 29360128 | tf_op jit(solution)/shard_map/moments_low/pallas_call | solution.py:366
  682.9 6.3 share_low.1.ratio
  689.1 12.1 %weights_low.1 = (f32[12,131072]{1,0:T(8,128)}, bf16[8,131072]{1,0:T(8,128)(2,1)}) custom-call(f32[12,131072]{1,0:T(8,128)} %w.9, f32[8,131072]{1,0:T(8,128)} %get-tuple-element.46.u, f32[8,128]{1,0:T(8,128)} %share_low.1.ratio, f32[12,131072]{1,0:T(8,128)} %get-tuple-element.50.refs_0_), custom_call_target="tpu_custom_call", output_to_operand_aliasing={{0}: (3, {})} | custom-call | flops 16777216 | bytes 16777216 | tf_op jit(solution)/shard_map/weights_low/pallas_call | solution.py:427
  701.3 0.0 all-gather.13.cloned.1.call-update
  701.3 0.0 all-gather.23.cloned.1.call-start
  701.3 54.7 %moments_mlp.1 = (f32[6,524288]{1,0:T(8,128)}, f32[6,524288]{1,0:T(8,128)}, f32[8,524288]{1,0:T(8,128)}, f32[16,128]{1,0:T(8,128)}) custom-call(f32[6,524288]{1,0:T(8,128)} %get-tuple-element.53.g, f32[6,524288]{1,0:T(8,128)} %w.11, f32[6,524288]{1,0:T(8,128)} %m.5, f32[6,524288]{1,0:T(8,128)} %v.5, f32[8,128]{1,0:T(8,128)} %copy-done.1), custom_call_target="tpu_custom_call" | custom-call | flops 117440512 | bytes 117440512 | tf_op jit(solution)/shard_map/moments_mlp/pallas_call | solution.py:366
  756.1 6.4 share_mlp.1.ratio
  762.5 34.1 %weights_mlp.1 = (f32[6,524288]{1,0:T(8,128)}, bf16[8,147456]{1,0:T(8,128)(2,1)}, bf16[8,122880]{1,0:T(8,128)(2,1)}, bf16[8,73728]{1,0:T(8,128)(2,1)}, bf16[8,49152]{1,0:T(8,128)(2,1)}) custom-call(f32[6,524288]{1,0:T(8,128)} %w.11, f32[8,524288]{1,0:T(8,128)} %get-tuple-element.54.u, f32[8,128]{1,0:T(8,128)} %share_mlp.1.ratio), custom_call_target="tpu_custom_call" | custom-call | flops 67108864 | bytes 67108864 | tf_op jit(solution)/shard_map/weights_mlp/pallas_call | solution.py:427
  796.6 0.0 all-gather.23.cloned.1.call-update
  796.7 0.0 all-gather.21.cloned.1.call-start
  796.7 0.5 all-gather.21.cloned.1.call-update
  797.3 0.0 all-gather.19.cloned.1.call-start
  797.3 0.5 all-gather.19.cloned.1.call-update
  797.8 0.0 all-gather.17.cloned.1.call-start
  797.9 0.5 all-gather.17.cloned.1.call-update
  798.4 1.2 slice.18
  800.3 0.8 multiply_reduce_fusion.2
  801.1 0.1 multiply_reduce_fusion.1
  801.3 0.7 fusion.part
  802.0 6.6 share_small.1
  808.5 0.8 rsqrt_multiply_fusion
  809.3 0.1 slice_multiply_fusion
  809.4 0.7 fusion.1
  810.1 11.5 %all_gather.55 = bf16[29,1024]{1,0:T(8,128)(2,1)} all-gather(bf16[29,128]{1,0:T(8,128)(2,1)S(1)} %get-tuple-element.70), channel_id=1, replica_groups=mesh['data'=8] {'data'}, dimensions={1}, use_global_device_ids=true | all-gather | bytes 66816 | tf_op jit(solution)/shard_map/all_gather | solution.py:537
  821.7 0.7 fusion.2
  822.3 11.6 %all_gather.54 = bf16[3,4096]{1,0:T(4,128)(2,1)} all-gather(bf16[3,512]{1,0:T(4,128)(2,1)S(1)} %get-tuple-element.72), channel_id=1, replica_groups=mesh['data'=8] {'data'}, dimensions={1}, use_global_device_ids=true | all-gather | bytes 27648 | tf_op jit(solution)/shard_map/all_gather | solution.py:537
  834.0 0.0 all-gather.13.cloned.1.call-done
  834.0 71.3 %unpack_attn.1 = bf16[12,1048576]{1,0:T(8,128)(2,1)} custom-call(bf16[8,8,131072]{2,1,0:T(8,128)(2,1)} %bitcast.11, bf16[8,8,65536]{2,1,0:T(8,128)(2,1)} %bitcast.14), custom_call_target="tpu_custom_call" | custom-call | flops 50331648 | bytes 50331648 | tf_op jit(solution)/shard_map/unpack_attn/pallas_call | solution.py:454
  905.4 0.0 all-gather.23.cloned.1.call-done
  905.4 54.8 %unpack_mlp_0.1.refs_0_ = bf16[6,4194304]{1,0:T(8,128)(2,1)} custom-call(bf16[8,8,147456]{2,1,0:T(8,128)(2,1)} %bitcast.10), custom_call_target="tpu_custom_call" | custom-call | flops 37748736 | bytes 37748736 | tf_op jit(solution)/shard_map/unpack_mlp_0/pallas_call | solution.py:480
  960.2 17.9 %all-gather.21.cloned.1.call-done = bf16[64,122880]{1,0:T(8,128)(2,1)} async-done(((bf16[8,122880]{1,0:T(8,128)(2,1)}), bf16[64,122880]{1,0:T(8,128)(2,1)}) %all-gather.21.cloned.1.call-update) | async-done | bytes 15728656 | tf_op jit(solution)/shard_map/all_gather | solution.py:519
  978.1 45.8 %unpack_mlp_12.1.refs_0_ = bf16[6,4194304]{1,0:T(8,128)(2,1)} custom-call(bf16[8,8,122880]{2,1,0:T(8,128)(2,1)} %bitcast.12, bf16[6,4194304]{1,0:T(8,128)(2,1)} %unpack_mlp_0.1.refs_0_), custom_call_target="tpu_custom_call", output_to_operand_aliasing={{}: (1, {})} | custom-call | flops 31457280 | bytes 31457280 | tf_op jit(solution)/shard_map/unpack_mlp_12/pallas_call | solution.py:480
  1023.9 8.8 all-gather.19.cloned.1.call-done
  1032.7 28.0 %unpack_mlp_22.1.refs_0_ = bf16[6,4194304]{1,0:T(8,128)(2,1)} custom-call(bf16[8,8,73728]{2,1,0:T(8,128)(2,1)} %bitcast.13, bf16[6,4194304]{1,0:T(8,128)(2,1)} %unpack_mlp_12.1.refs_0_), custom_call_target="tpu_custom_call", output_to_operand_aliasing={{}: (1, {})} | custom-call | flops 18874368 | bytes 18874368 | tf_op jit(solution)/shard_map/unpack_mlp_22/pallas_call | solution.py:480
  1060.7 13.3 %all-gather.17.cloned.1.call-done = bf16[64,49152]{1,0:T(8,128)(2,1)} async-done(((bf16[8,49152]{1,0:T(8,128)(2,1)}), bf16[64,49152]{1,0:T(8,128)(2,1)}) %all-gather.17.cloned.1.call-update) | async-done | bytes 6291472 | tf_op jit(solution)/shard_map/all_gather | solution.py:519
  1073.9 19.0 %unpack_mlp_28.1 = bf16[6,4194304]{1,0:T(8,128)(2,1)} custom-call(bf16[8,8,49152]{2,1,0:T(8,128)(2,1)} %bitcast.15, bf16[6,4194304]{1,0:T(8,128)(2,1)} %unpack_mlp_22.1.refs_0_), custom_call_target="tpu_custom_call", output_to_operand_aliasing={{}: (1, {})} | custom-call | flops 12582912 | bytes 12582912 | tf_op jit(solution)/shard_map/unpack_mlp_28/pallas_call | solution.py:480
  1093.0 0.6 copy.46
  1093.6 0.6 copy.47
  (25 shorter events, 0.1 us)
Async XLA Ops:
  7.2 826.8 %all-gather.15.cloned.1.call-start = ((), (), s32[]{:S(2)}) async-start(), calls=%async_computation.1 | async-start | bytes 9437184 | tf_op jit(solution)/shard_map/all_gather | solution.py:509
  7.2 0.8 copy-start
  8.1 0.8 copy-start.2
  628.3 0.6 copy-start.1
  665.1 168.9 %all-gather.13.cloned.1.call-start = ((), (), s32[]{:S(2)}) async-start(), calls=%async_computation | async-start | bytes 18874368 | tf_op jit(solution)/shard_map/all_gather | solution.py:514
  701.3 204.1 %all-gather.23.cloned.1.call-start = ((), (), s32[]{:S(2)}) async-start(), calls=%async_computation.5 | async-start | bytes 21233664 | tf_op jit(solution)/shard_map/all_gather | solution.py:519
  762.5 37.8 %copy-start.8 = (f32[3,512]{1,0:T(4,128)S(1)}, f32[3,512]{1,0:T(4,128)}, u32[]{:S(2)}) copy-start(f32[3,512]{1,0:T(4,128)} %param.22) | copy-start | bytes 18436
  762.5 37.8 %copy-start.11 = (f32[3,512]{1,0:T(4,128)S(1)}, f32[3,512]{1,0:T(4,128)}, u32[]{:S(2)}) copy-start(f32[3,512]{1,0:T(4,128)} %param.26) | copy-start | bytes 18436
  762.5 37.8 %copy-start.12 = (f32[3,512]{1,0:T(4,128)S(1)}, f32[3,512]{1,0:T(4,128)}, u32[]{:S(2)}) copy-start(f32[3,512]{1,0:T(4,128)} %param.30) | copy-start | bytes 18436
  762.5 38.6 %copy-start.5 = (f32[29,128]{1,0:T(8,128)S(1)}, f32[29,128]{1,0:T(8,128)}, u32[]{:S(2)}) copy-start(f32[29,128]{1,0:T(8,128)} %param.23) | copy-start | bytes 44548
  762.5 38.6 %copy-start.9 = (f32[29,128]{1,0:T(8,128)S(1)}, f32[29,128]{1,0:T(8,128)}, u32[]{:S(2)}) copy-start(f32[29,128]{1,0:T(8,128)} %param.27) | copy-start | bytes 44548
  762.5 38.6 %copy-start.10 = (f32[29,128]{1,0:T(8,128)S(1)}, f32[29,128]{1,0:T(8,128)}, u32[]{:S(2)}) copy-start(f32[29,128]{1,0:T(8,128)} %param.31) | copy-start | bytes 44548
  796.7 181.4 %all-gather.21.cloned.1.call-start = ((), (), s32[]{:S(2)}) async-start(), calls=%async_computation.4 | async-start | bytes 17694720 | tf_op jit(solution)/shard_map/all_gather | solution.py:519
  797.3 235.5 %all-gather.19.cloned.1.call-start = ((), (), s32[]{:S(2)}) async-start(), calls=%async_computation.3 | async-start | bytes 10616832 | tf_op jit(solution)/shard_map/all_gather | solution.py:519
  797.8 276.1 %all-gather.17.cloned.1.call-start = ((), (), s32[]{:S(2)}) async-start(), calls=%async_computation.2 | async-start | bytes 7077888 | tf_op jit(solution)/shard_map/all_gather | solution.py:519
  801.3 104.1 %copy-start.6 = (f32[29,128]{1,0:T(8,128)}, f32[29,128]{1,0:T(8,128)S(1)}, u32[]{:S(2)}) copy-start(f32[29,128]{1,0:T(8,128)S(1)} %get-tuple-element.108) | copy-start | bytes 44548
  801.3 104.1 %copy-start.7 = (f32[29,128]{1,0:T(8,128)}, f32[29,128]{1,0:T(8,128)S(1)}, u32[]{:S(2)}) copy-start(f32[29,128]{1,0:T(8,128)S(1)} %get-tuple-element.112) | copy-start | bytes 44548
  1073.9 19.0 %copy-start.4 = (bf16[3,4096]{1,0:T(4,128)(2,1)S(1)}, bf16[3,4096]{1,0:T(4,128)(2,1)}, u32[]{:S(2)}) copy-start(bf16[3,4096]{1,0:T(4,128)(2,1)} %all_gather.54) | copy-start | bytes 73732
  1073.9 19.7 %copy-start.3 = (bf16[29,1024]{1,0:T(8,128)(2,1)S(1)}, bf16[29,1024]{1,0:T(8,128)(2,1)}, u32[]{:S(2)}) copy-start(bf16[29,1024]{1,0:T(8,128)(2,1)} %all_gather.55) | copy-start | bytes 178180
Sparse Core Ops, SparseCore 0:
  665.2 48.3 all-gather.14
  715.4 84.7 all-gather.12
  802.6 94.1 all-gather.22
  898.4 79.6 all-gather.20
  979.7 52.9 all-gather.18
  1034.4 39.5 all-gather.16
